TPU v7x, 512 devices: a whole 4x4x16 slice. The times are simulated.
512 devices in a mesh: grp: 32 (over z, core), dev: 16 (over y, x).
Axes of the slice: x: 4, y: 4, z: 16, core: 2. Of those that a mesh axis runs over, the one named last changes fastest.
Arguments:
- sketch: float32 [524288, 512], P(('grp', 'dev')), may hold values from -50 to 50
- row_counts: int32 [512], P(('grp', 'dev')), may hold values from 0 to 1024, as said below
Outputs:
- q_factor: float32 [524288, 512], P(('grp', 'dev'))
- r_factor: float32 [512, 512], P('dev')
Inputs may be any that keep to these rules, and one draw needn't show every extreme that they name: `row_counts`: every entry is a multiple of 128. Each aligned group of 16 consecutive entries sums to 4096, and in each such group at least one entry equals 1024.
All inputs are finite; a program needn't handle non-finite values.
Results may differ from a plain program's by a relative error of at most 0.00015.
Values sent between devices are 32-bit elements; how exact they have to be, the bound alone decides.
No kernel may reach another device: no remote copies, remote signals or barrier semaphores. Data moves between devices by JAX's collectives and lax.ppermute only.
A program may use at most 128 MiB of HBM per device.

v0:
```python
import jax
import jax.numpy as jnp
from jax import lax
from jax.sharding import Mesh
from jax.sharding import PartitionSpec as P

SLOTS = 16
HOLD = 4
DEV = ("dev_0", "dev_1")
GRP = ("grp_0", "grp_1")
GRP_DEV = ("grp_0", "grp_1", "dev_0", "dev_1")


def split_up(value, dim, devices):
    before, after = (value.shape[:dim], value.shape[dim + 1 :])
    return jnp.moveaxis(value.reshape(*before, devices, -1, *after), dim, 0)


def sum_at_owner(value, axis, dim):
    tiles = split_up(value, dim, lax.axis_size(axis))
    arrived = lax.all_to_all(tiles, axis, split_axis=0, concat_axis=0, tiled=True)
    return arrived.sum(axis=0)


def sum_in_two_steps(value, axes, dim):
    far, near = axes
    own = sum_at_owner(split_up(value, dim, lax.axis_size(far)), near, dim + 1)
    return jnp.sum(lax.all_to_all(own, far, 0, 0, tiled=True), axis=0)


def padded_to(lines, devices):
    spare = -lines.shape[0] % devices
    if not spare:
        return lines
    return jnp.concatenate([lines, jnp.zeros((spare, *lines.shape[1:]), lines.dtype)])


def from_everyone(value, axis):
    copies = jnp.broadcast_to(value, (lax.axis_size(axis), *value.shape))
    return lax.all_to_all(copies, axis, split_axis=0, concat_axis=0, tiled=True)


def joined_along(tiles, dim):
    tiles = jnp.moveaxis(tiles, 0, dim)
    shape = tiles.shape
    return tiles.reshape(*shape[:dim], shape[dim] * shape[dim + 1], *shape[dim + 2 :])


def gathered_by_axis(value, axes, dim):
    far, near = axes
    tiles = from_everyone(from_everyone(value, far), near)
    return joined_along(tiles.swapaxes(0, 1).reshape(-1, *value.shape), dim)


def nested_sum(value, axes):
    lines = value.reshape(-1, value.shape[-1])
    own = sum_in_two_steps(
        padded_to(lines, lax.axis_size(axes[0]) * lax.axis_size(axes[1])), axes, 0
    )
    whole = gathered_by_axis(own, axes, 0)
    return whole[: len(lines)].reshape(value.shape)


def matmul(left, right):
    return jnp.dot(left, right, precision=lax.Precision.HIGHEST)


def gram_of(rows_in):
    return lax.dot_general(
        rows_in, rows_in, (((0,), (0,)), ((), ())), precision=lax.Precision.HIGHEST
    )


def lower_and_inverse(matrix):
    order = matrix.shape[0]
    if order == 1:
        root = jnp.sqrt(matrix)
        return (root, 1.0 / root)
    half = order // 2
    lower_top, inverse_top = lower_and_inverse(matrix[:half, :half])
    lower_left = matmul(matrix[half:, :half], inverse_top.T)
    schur = matrix[half:, half:] - matmul(lower_left, lower_left.T)
    lower_bottom, inverse_bottom = lower_and_inverse(schur)
    inverse_left = -matmul(inverse_bottom, matmul(lower_left, inverse_top))
    zeros_top = jnp.zeros((half, order - half), jnp.float32)
    lower = jnp.concatenate(
        [
            jnp.concatenate([lower_top, zeros_top], axis=1),
            jnp.concatenate([lower_left, lower_bottom], axis=1),
        ],
        axis=0,
    )
    inverse = jnp.concatenate(
        [
            jnp.concatenate([inverse_top, zeros_top], axis=1),
            jnp.concatenate([inverse_left, inverse_bottom], axis=1),
        ],
        axis=0,
    )
    return (lower, inverse)


def shards(sketch, row_counts):
    capacity, columns = sketch.shape
    block_rows = capacity // SLOTS
    members = lax.axis_size(DEV)
    own_index = lax.axis_index(DEV)
    row_total = lax.axis_size(GRP) * members * HOLD * block_rows
    own_count = row_counts[0]
    inside = jnp.arange(capacity, dtype=jnp.int32) < own_count
    own_rows = jnp.where(inside[:, None], sketch, jnp.zeros((), sketch.dtype))
    gram_sum = nested_sum(gram_of(own_rows), (("grp_0", "grp_1"), ("dev_0", "dev_1")))
    lower, inverse = lower_and_inverse(gram_sum / row_total)
    upper_factor = lower.T
    upper_inverse = inverse.T
    share = columns // members
    r_rows = lax.dynamic_slice_in_dim(upper_factor, own_index * share, share, 0)
    q_rows = matmul(own_rows, upper_inverse)
    return (q_rows, r_rows)


def solution(mesh):
    finer = Mesh(mesh.devices.reshape(16, 2, 4, 4), ("grp_0", "grp_1", "dev_0", "dev_1"))
    placed = (P(GRP_DEV, None), P(GRP_DEV))
    return jax.shard_map(
        shards,
        mesh=finer,
        in_specs=placed,
        out_specs=(P(GRP_DEV, None), P(DEV, None)),
        check_vma=False,
    )
```

profile of v0, /device:TPU:1, one launch (start us, length us, event | category | flops | bytes accessed | tf_op | source)
XLA Modules:
  0.0 1002.8 jit_solution(7481134967663237821)
XLA Ops:
  1.3 6.4 fusion.2
  8.3 22.7 %all_to_all.23 = f32[16,32,1,512]{3,1,2,0:T(8,128)S(1)} all-to-all(f32[16,32,1,512]{3,1,2,0:T(8,128)S(1)} %bitcast.3080), channel_id=1, replica_groups=mesh['grp_0'=16,'grp_1'=2,'dev_0'=4,'dev_1'=4] {'dev_0','dev_1'}, dimensions={0} | all-to-all | bytes 2097152 | tf_op jit(solution)/shard_map/all_to_all | solution.py:21
  31.2 30.8 %all_to_all.24 = f32[32,1,512]{2,1,0:T(1,128)S(1)} all-to-all(f32[32,1,512]{2,1,0:T(1,128)S(1)} %reduce_sum.21), channel_id=1, replica_groups=mesh['grp_0'=16,'grp_1'=2,'dev_0'=4,'dev_1'=4] {'grp_0','grp_1'}, dimensions={0} | all-to-all | bytes 131072 | tf_op jit(solution)/shard_map/all_to_all | solution.py:28
  62.1 17.2 %all_to_all.25 = f32[32,1,512]{2,1,0:T(1,128)S(1)} all-to-all(f32[32,1,512]{2,1,0:T(1,128)S(1)} %broadcast_in_dim.22), channel_id=1, replica_groups=mesh['grp_0'=16,'grp_1'=2,'dev_0'=4,'dev_1'=4] {'grp_0','grp_1'}, dimensions={0} | all-to-all | bytes 131072 | tf_op jit(solution)/shard_map/all_to_all | solution.py:40
  79.4 1.1 broadcast_in_dim.23
  80.5 3.9 all-to-all-start.3
  84.6 14.8 %all-to-all-done.3 = f32[16,32,1,512]{3,1,2,0:T(8,128)S(1)} async-done(((f32[16,32,1,512]{3,1,2,0:T(8,128)}), f32[16,32,1,512]{3,1,2,0:T(8,128)S(1)}, u32[]{:S(2)}, u32[]{:S(2)}) %all-to-all-start.3) | async-done | bytes 1048608 | tf_op jit(solution)/shard_map/all_to_all | solution.py:40
  110.0 0.7 fusion.5164
  164.8 0.7 fusion.5156
  168.5 0.7 fusion.4971
  171.9 0.7 fusion.5155
  175.4 0.7 fusion.5032
  287.1 0.7 fusion.5138
  291.1 0.7 fusion.4938
  294.4 0.7 fusion.5137
  297.9 0.7 fusion.5023
  301.2 0.7 fusion.5136
  305.0 0.7 fusion.4966
  308.3 0.7 fusion.5135
  311.9 0.7 fusion.5022
  357.6 0.7 fusion.5128
  361.4 0.7 fusion.4964
  364.7 0.7 fusion.5127
  368.2 0.7 fusion.5018
  402.5 0.7 fusion.4936
  454.6 0.7 fusion.5114
  458.5 0.7 fusion.4935
  461.9 0.7 fusion.5113
  465.4 0.7 fusion.5011
  988.3 3.8 fusion.32
  993.4 0.7 copy.527
  996.2 6.5 fusion
  (2070 shorter events, 348.2 us)
Async XLA Ops:
  80.5 19.0 %all-to-all-start.3 = ((f32[16,32,1,512]{3,1,2,0:T(8,128)}), f32[16,32,1,512]{3,1,2,0:T(8,128)S(1)}, u32[]{:S(2)}, u32[]{:S(2)}) async-start(f32[16,32,1,512]{3,1,2,0:T(8,128)} %broadcast_in_dim.23), calls=%async_computation.3 | async-start | bytes 2097152 | tf_op jit(solution)/shard_map/all_to_all | solution.py:40
  454.3 23.9 %copy-start.42 = (f32[2,2]{1,0:T(2,128)}, f32[2,2]{1,0:T(2,128)S(1)}, u32[]{:S(2)}) copy-start(f32[2,2]{1,0:T(2,128)S(1)} %fusion.4573) | copy-start | bytes 52
  550.7 142.0 %copy-start.58 = (f32[2,2]{1,0:T(2,128)}, f32[2,2]{1,0:T(2,128)S(1)}, u32[]{:S(2)}) copy-start(f32[2,2]{1,0:T(2,128)S(1)} %fusion.4553) | copy-start | bytes 52
  962.1 23.3 %copy-start.21 = (f32[2,2]{1,0:T(2,128)S(1)}, f32[2,2]{1,0:T(2,128)}, u32[]{:S(2)}) copy-start(f32[2,2]{1,0:T(2,128)} %copy-done.20) | copy-start | bytes 52
  962.1 23.4 %copy-start.25 = (f32[2,2]{1,0:T(2,128)S(1)}, f32[2,2]{1,0:T(2,128)}, u32[]{:S(2)}) copy-start(f32[2,2]{1,0:T(2,128)} %copy-done.24) | copy-start | bytes 52
  962.1 23.4 %copy-start.27 = (f32[2,2]{1,0:T(2,128)S(1)}, f32[2,2]{1,0:T(2,128)}, u32[]{:S(2)}) copy-start(f32[2,2]{1,0:T(2,128)} %copy-done.26) | copy-start | bytes 52
  962.2 23.5 %copy-start.31 = (f32[2,2]{1,0:T(2,128)S(1)}, f32[2,2]{1,0:T(2,128)}, u32[]{:S(2)}) copy-start(f32[2,2]{1,0:T(2,128)} %copy-done.30) | copy-start | bytes 52
  962.2 23.6 %copy-start.35 = (f32[2,2]{1,0:T(2,128)S(1)}, f32[2,2]{1,0:T(2,128)}, u32[]{:S(2)}) copy-start(f32[2,2]{1,0:T(2,128)} %copy-done.34) | copy-start | bytes 52
  962.2 23.7 %copy-start.39 = (f32[2,2]{1,0:T(2,128)S(1)}, f32[2,2]{1,0:T(2,128)}, u32[]{:S(2)}) copy-start(f32[2,2]{1,0:T(2,128)} %copy-done.38) | copy-start | bytes 52
  962.2 23.8 %copy-start.41 = (f32[2,2]{1,0:T(2,128)S(1)}, f32[2,2]{1,0:T(2,128)}, u32[]{:S(2)}) copy-start(f32[2,2]{1,0:T(2,128)} %copy-done.40) | copy-start | bytes 52
  962.2 23.8 %copy-start.45 = (f32[2,2]{1,0:T(2,128)S(1)}, f32[2,2]{1,0:T(2,128)}, u32[]{:S(2)}) copy-start(f32[2,2]{1,0:T(2,128)} %copy-done.44) | copy-start | bytes 52
  962.2 23.9 %copy-start.49 = (f32[2,2]{1,0:T(2,128)S(1)}, f32[2,2]{1,0:T(2,128)}, u32[]{:S(2)}) copy-start(f32[2,2]{1,0:T(2,128)} %copy-done.48) | copy-start | bytes 52
  962.2 24.0 %copy-start.53 = (f32[2,2]{1,0:T(2,128)S(1)}, f32[2,2]{1,0:T(2,128)}, u32[]{:S(2)}) copy-start(f32[2,2]{1,0:T(2,128)} %copy-done.52) | copy-start | bytes 52
  962.2 24.1 %copy-start.55 = (f32[2,2]{1,0:T(2,128)S(1)}, f32[2,2]{1,0:T(2,128)}, u32[]{:S(2)}) copy-start(f32[2,2]{1,0:T(2,128)} %copy-done.54) | copy-start | bytes 52
  962.2 24.3 %copy-start.57 = (f32[2,2]{1,0:T(2,128)S(1)}, f32[2,2]{1,0:T(2,128)}, u32[]{:S(2)}) copy-start(f32[2,2]{1,0:T(2,128)} %copy-done.56) | copy-start | bytes 52
  962.2 24.4 %copy-start.65 = (f32[2,2]{1,0:T(2,128)S(1)}, f32[2,2]{1,0:T(2,128)}, u32[]{:S(2)}) copy-start(f32[2,2]{1,0:T(2,128)} %copy-done.64) | copy-start | bytes 52
  962.3 24.5 %copy-start.71 = (f32[2,2]{1,0:T(2,128)S(1)}, f32[2,2]{1,0:T(2,128)}, u32[]{:S(2)}) copy-start(f32[2,2]{1,0:T(2,128)} %copy-done.70) | copy-start | bytes 52
  962.3 24.6 %copy-start.79 = (f32[2,2]{1,0:T(2,128)S(1)}, f32[2,2]{1,0:T(2,128)}, u32[]{:S(2)}) copy-start(f32[2,2]{1,0:T(2,128)} %copy-done.78) | copy-start | bytes 52
  962.3 24.6 %copy-start.3 = (f32[2,2]{1,0:T(2,128)S(1)}, f32[2,2]{1,0:T(2,128)}, u32[]{:S(2)}) copy-start(f32[2,2]{1,0:T(2,128)} %copy-done.2) | copy-start | bytes 52
  962.3 24.7 %copy-start.9 = (f32[2,2]{1,0:T(2,128)S(1)}, f32[2,2]{1,0:T(2,128)}, u32[]{:S(2)}) copy-start(f32[2,2]{1,0:T(2,128)} %copy-done.8) | copy-start | bytes 52
  962.3 24.8 %copy-start.15 = (f32[2,2]{1,0:T(2,128)S(1)}, f32[2,2]{1,0:T(2,128)}, u32[]{:S(2)}) copy-start(f32[2,2]{1,0:T(2,128)} %copy-done.14) | copy-start | bytes 52
  962.3 24.9 %copy-start.23 = (f32[2,2]{1,0:T(2,128)S(1)}, f32[2,2]{1,0:T(2,128)}, u32[]{:S(2)}) copy-start(f32[2,2]{1,0:T(2,128)} %copy-done.22) | copy-start | bytes 52
  962.3 25.0 %copy-start.29 = (f32[2,2]{1,0:T(2,128)S(1)}, f32[2,2]{1,0:T(2,128)}, u32[]{:S(2)}) copy-start(f32[2,2]{1,0:T(2,128)} %copy-done.28) | copy-start | bytes 52
  962.3 25.1 %copy-start.37 = (f32[2,2]{1,0:T(2,128)S(1)}, f32[2,2]{1,0:T(2,128)}, u32[]{:S(2)}) copy-start(f32[2,2]{1,0:T(2,128)} %copy-done.36) | copy-start | bytes 52
  962.3 25.1 %copy-start.43 = (f32[2,2]{1,0:T(2,128)S(1)}, f32[2,2]{1,0:T(2,128)}, u32[]{:S(2)}) copy-start(f32[2,2]{1,0:T(2,128)} %copy-done.42) | copy-start | bytes 52
  962.3 25.2 %copy-start.51 = (f32[2,2]{1,0:T(2,128)S(1)}, f32[2,2]{1,0:T(2,128)}, u32[]{:S(2)}) copy-start(f32[2,2]{1,0:T(2,128)} %copy-done.50) | copy-start | bytes 52
  962.4 25.4 %copy-start.61 = (f32[2,2]{1,0:T(2,128)S(1)}, f32[2,2]{1,0:T(2,128)}, u32[]{:S(2)}) copy-start(f32[2,2]{1,0:T(2,128)} %copy-done.60) | copy-start | bytes 52
  962.4 25.5 %copy-start.75 = (f32[2,2]{1,0:T(2,128)S(1)}, f32[2,2]{1,0:T(2,128)}, u32[]{:S(2)}) copy-start(f32[2,2]{1,0:T(2,128)} %copy-done.74) | copy-start | bytes 52
  962.4 25.6 %copy-start.5 = (f32[2,2]{1,0:T(2,128)S(1)}, f32[2,2]{1,0:T(2,128)}, u32[]{:S(2)}) copy-start(f32[2,2]{1,0:T(2,128)} %copy-done.4) | copy-start | bytes 52
  962.4 25.6 %copy-start.19 = (f32[2,2]{1,0:T(2,128)S(1)}, f32[2,2]{1,0:T(2,128)}, u32[]{:S(2)}) copy-start(f32[2,2]{1,0:T(2,128)} %copy-done.18) | copy-start | bytes 52
  962.4 25.7 %copy-start.33 = (f32[2,2]{1,0:T(2,128)S(1)}, f32[2,2]{1,0:T(2,128)}, u32[]{:S(2)}) copy-start(f32[2,2]{1,0:T(2,128)} %copy-done.32) | copy-start | bytes 52
  962.7 25.5 %copy-start.47 = (f32[2,2]{1,0:T(2,128)S(1)}, f32[2,2]{1,0:T(2,128)}, u32[]{:S(2)}) copy-start(f32[2,2]{1,0:T(2,128)} %copy-done.46) | copy-start | bytes 52
  (51 other events, 385.2 us)
where the time goes:
time: 1020 us; the launch traced here: 1000 us
  between operations  530 us (52%)
  local copies, waits for them, and re-layouts  176 us (17%)
  matrix products  160 us (16%)
  blocking collectives  70.8 us (7%)
  other arithmetic  46.7 us (5%)
  waiting for transfers between devices  14.8 us (1%)
    slice x256, local copies, waits for them, and re-layouts, lower_and_inverse(): lower_top, inverse_top = lower_and_inverse(matrix[:half, :half])  170 us
    dot_general x1021, matrix products, matmul(): return jnp.dot(left, right, precision=lax.Precision.HIGHEST)  153 us
    all_to_all x1, blocking collectives, sum_in_two_steps(): return jnp.sum(lax.all_to_all(own, far, 0, 0, tiled=True), axis=0)  30.8 us
    concatenate x258, other arithmetic, lower_and_inverse(): jnp.concatenate([jnp.concatenate([lower_top, zeros_top], axis=1), jnp.con...  24.6 us
    all_to_all x1, blocking collectives, sum_at_owner(): lax.all_to_all(tiles, axis, split_axis=0, concat_axis=0, tiled=True)  22.7 us
    concatenate x255, other arithmetic, lower_and_inverse(): jnp.concatenate([jnp.concatenate([inverse_top, zeros_top], axis=1), jnp.c...  21.1 us
  transfers between devices with their start and end apart: 1, of which 1 were waited for; matrix products, arithmetic and copies ran while one was open for 0% of the time, Pallas kernels for 0%

commit v1 on v0

v1 whole, which is shorter than its diff:
```python
import functools

import jax
import jax.numpy as jnp
from jax import lax
from jax.experimental import pallas as pl
from jax.experimental.pallas import tpu as pltpu
from jax.sharding import Mesh
from jax.sharding import PartitionSpec as P

SLOTS = 16
HOLD = 4
B = 128
NB = 32
SUB = 8
DEV = ("y", "x")
ALL = ("z", "core", "y", "x")
HIGH = lax.Precision.HIGHEST
WHOLE = pl.BlockSpec(memory_space=pltpu.VMEM)


def dot(left, right, dims=((1,), (0,))):
    return lax.dot_general(
        left, right, (dims, ((), ())), precision=HIGH, preferred_element_type=jnp.float32
    )


def upper_blocks(order):
    count = order // B
    return [(i, j) for i in range(count) for j in range(i, count)]


def gram_kernel(count_ref, rows_ref, packed_ref):
    capacity, order = rows_ref.shape
    row = lax.broadcasted_iota(jnp.int32, (capacity, order), 0)
    live = jnp.where(row < count_ref[0], rows_ref[...], 0.0)
    at = 0
    for i in range(order // B):
        wide = dot(live[:, i * B : (i + 1) * B], live[:, i * B :], ((0,), (0,)))
        for j in range(order // B - i):
            packed_ref[at : at + B, :] = wide[:, j * B : (j + 1) * B]
            at += B


def gram_of(rows_in, count):
    order = rows_in.shape[1]
    return pl.pallas_call(
        gram_kernel,
        out_shape=jax.ShapeDtypeStruct((len(upper_blocks(order)) * B, B), jnp.float32),
        in_specs=[pl.BlockSpec(memory_space=pltpu.SMEM), WHOLE],
        out_specs=WHOLE,
        name="gram",
    )(count, rows_in)


def spread(row):
    return jnp.broadcast_to(row, (SUB, row.shape[1]))


def eliminate(strip, at):
    groups = NB // SUB
    lane = lax.broadcasted_iota(jnp.int32, (SUB, B), 1)
    sub = lax.broadcasted_iota(jnp.int32, (SUB, B), 0)
    raw = [strip[v * SUB : (v + 1) * SUB] for v in range(groups)]
    diagonal = (lane >= at) & (lane < at + NB)
    aug = [
        jnp.where(diagonal, (lane == sub + (at + v * SUB)).astype(jnp.float32), raw[v])
        for v in range(groups)
    ]
    cols = [
        [
            None
            if v < j // SUB
            else jnp.broadcast_to(raw[v][:, at + j : at + j + 1], (SUB, B))
            for v in range(groups)
        ]
        for j in range(NB)
    ]
    for j in range(NB):
        first, r = divmod(j, SUB)
        root = lax.rsqrt(spread(cols[j][first][r : r + 1]))
        scaled = [None if c is None else c * root for c in cols[j]]
        row_raw = spread(raw[first][r : r + 1]) * root
        row_aug = spread(aug[first][r : r + 1]) * root
        below = jnp.where(sub > r, scaled[first], 0.0)
        raw[first] = jnp.where(sub == r, row_raw, raw[first] - below * row_raw)
        aug[first] = jnp.where(sub == r, row_aug, aug[first] - below * row_aug)
        for v in range(first + 1, groups):
            raw[v] = raw[v] - scaled[v] * row_raw
            aug[v] = aug[v] - scaled[v] * row_aug
        for l in range(j + 1, NB):
            g, q = divmod(l, SUB)
            factor = spread(scaled[g][q : q + 1])
            for v in range(g, groups):
                cols[l][v] = cols[l][v] - scaled[v] * factor
        cols[j] = None
    return jnp.concatenate(raw), jnp.concatenate(aug)


def factor_block(block):
    strips = [block[b * NB : (b + 1) * NB] for b in range(B // NB)]
    lane = lax.broadcasted_iota(jnp.int32, (NB, B), 1)
    sub = lax.broadcasted_iota(jnp.int32, (NB, B), 0)
    upper, inverse = [], []
    for b in range(B // NB):
        at = b * NB
        raw, aug = eliminate(strips[b], at)
        upper.append(jnp.where(lane >= sub + at, raw, 0.0))
        inverse.append(jnp.where(lane <= sub + at, aug, 0.0))
        if at + NB < B:
            change = dot(raw.T[at + NB :], aug)
            hit = (lane >= at) & (lane < at + NB)
            for i in range(b + 1, B // NB):
                o = (i - b - 1) * NB
                strips[i] = jnp.where(hit, 0.0, strips[i]) - change[o : o + NB]
    return jnp.concatenate(upper), jnp.concatenate(inverse)


def factor_kernel(scale, packed_ref, upper_ref, inverse_ref, work):
    order = work.shape[0]
    for p, (i, j) in enumerate(upper_blocks(order)):
        work[i * B : (i + 1) * B, j * B : (j + 1) * B] = (
            packed_ref[p * B : (p + 1) * B, :] * scale
        )
    for s in range(order // B):
        lo, hi = s * B, (s + 1) * B
        here = slice(lo, hi)
        upper, inverse = factor_block(work[here, here])
        upper_ref[here, here] = upper
        inverse_ref[here, here] = inverse
        parts = []
        if lo:
            left = dot(inverse, work[here, :lo])
            inverse_ref[here, :lo] = left
            upper_ref[here, :lo] = jnp.zeros((B, lo), jnp.float32)
            parts.append(left)
        parts.append(inverse)
        if hi < order:
            right = dot(inverse, work[here, hi:])
            upper_ref[here, hi:] = right
            inverse_ref[here, hi:] = jnp.zeros((B, order - hi), jnp.float32)
            parts.append(right)
            change = dot(right.T, jnp.concatenate(parts, axis=1))
            if lo:
                work[hi:, :lo] = work[hi:, :lo] - change[:, :lo]
            work[hi:, here] = -change[:, here]
            work[hi:, hi:] = work[hi:, hi:] - change[:, hi:]


def factors_of(packed, order, scale):
    return pl.pallas_call(
        functools.partial(factor_kernel, scale),
        out_shape=[jax.ShapeDtypeStruct((order, order), jnp.float32)] * 2,
        in_specs=[WHOLE],
        out_specs=[WHOLE] * 2,
        scratch_shapes=[pltpu.VMEM((order, order), jnp.float32)],
        name="factor",
    )(packed)


def apply_kernel(count_ref, rows_ref, inverse_ref, out_ref):
    height, order = rows_ref.shape
    row = lax.broadcasted_iota(jnp.int32, (height, order), 0)
    start = pl.program_id(0) * height
    live = jnp.where(row + start < count_ref[0], rows_ref[...], 0.0)
    half = order // 2
    for k in range(2):
        hi = (k + 1) * half
        out_ref[:, k * half : hi] = dot(
            live[:, :hi], inverse_ref[k * half : hi, :hi], ((1,), (1,))
        )


def applied(rows_in, count, inverse):
    capacity, order = rows_in.shape
    height = capacity // 4
    tile = pl.BlockSpec((height, order), lambda i: (i, 0))
    return pl.pallas_call(
        apply_kernel,
        grid=(capacity // height,),
        out_shape=jax.ShapeDtypeStruct(rows_in.shape, jnp.float32),
        in_specs=[
            pl.BlockSpec(memory_space=pltpu.SMEM),
            tile,
            pl.BlockSpec((order, order), lambda i: (0, 0)),
        ],
        out_specs=tile,
        name="apply",
    )(count, rows_in, inverse)


def everyone(value, axis):
    copies = jnp.broadcast_to(value, (lax.axis_size(axis), *value.shape))
    return lax.all_to_all(copies, axis, split_axis=0, concat_axis=0, tiled=True)


def swapped(value):
    return lax.ppermute(value, "core", [(0, 1), (1, 0)])


def summed(packed):
    members = lax.axis_size(DEV)
    tiles = packed.reshape(members, -1, B)
    own = lax.all_to_all(tiles, DEV, split_axis=0, concat_axis=0, tiled=True).sum(axis=0)
    core = lax.axis_index("core")
    half = own.shape[0] // 2
    mine = lax.dynamic_slice_in_dim(own, core * half, half, 0)
    other = lax.dynamic_slice_in_dim(own, (1 - core) * half, half, 0)
    part = everyone(mine + swapped(other), "z").sum(axis=0)
    back = swapped(part)
    own = jnp.where(core == 0, jnp.stack([part, back]), jnp.stack([back, part]))
    return everyone(own.reshape(-1, B), DEV).reshape(-1, B)


def shards(sketch, row_counts):
    capacity, order = sketch.shape
    members = lax.axis_size(DEV)
    row_total = lax.axis_size(ALL) * HOLD * (capacity // SLOTS)
    packed = summed(gram_of(sketch, row_counts))
    upper, inverse = factors_of(packed, order, 1.0 / row_total)
    share = order // members
    r_rows = lax.dynamic_slice_in_dim(upper, lax.axis_index(DEV) * share, share, 0)
    return (applied(sketch, row_counts, inverse), r_rows)


def solution(mesh):
    finer = Mesh(mesh.devices.reshape(16, 2, 4, 4), ALL)
    return jax.shard_map(
        shards,
        mesh=finer,
        in_specs=(P(ALL, None), P(ALL)),
        out_specs=(P(ALL, None), P(DEV, None)),
        check_vma=False,
    )
```

time: 1020 us -> 114 us (0.11); the launches traced: 1000 us -> 113 us
  between operations: 530 us -> 1.35 us
  local copies, waits for them, and re-layouts: 176 us -> 3.23 us
  matrix products: 160 us -> 0 us
  other arithmetic: 46.7 us -> 0.07 us
  blocking collectives: 70.8 us -> 30.2 us
  Pallas kernels: 0 us -> 28.8 us
  starting transfers between devices: 3.95 us -> 25.2 us
    slice x256 -> x0, local copies, waits for them, and re-layouts: 170 us -> none  [lower_and_inverse(): lower_top, inverse_top = lower_and_inverse(matrix[:half, :half])]
    dot_general x1022 -> x0, matrix products: 160 us -> none  [the longest x1021 153 us: matmul(): return jnp.dot(left, right, precision=lax.Precision.HIGHEST)]
    concatenate x513 -> x0, other arithmetic: 45.7 us -> none  [the longest x258 24.6 us: lower_and_inverse(): jnp.concatenate([jnp.concatenate([lower_top, zeros_top], axis=1), jnp.con...]
    all_to_all x3 -> x1, blocking collectives: 70.8 us -> 30.2 us  [everyone(): return lax.all_to_all(copies, axis, split_axis=0, concat_axis=0, tiled=True)]
    pallas_call x0 -> x3, Pallas kernels: none -> 28.8 us  [the longest x1 17.4 us: factors_of(): pl.pallas_call(functools.partial(factor_kernel, scale), out_shape=[jax.Sh...]
    ppermute x0 -> x2, starting transfers between devices: none -> 13.9 us  [swapped(): return lax.ppermute(value, 'core', [(0, 1), (1, 0)])]
    all_to_all x1 -> x2, waiting for transfers between devices: 14.8 us -> 22.6 us  [the longest x1 12.2 us: everyone(): return lax.all_to_all(copies, axis, split_axis=0, concat_axis=0, tiled=True)]
  transfers between devices with their start and end apart: 1 -> 4, of which waited for: 1 -> 4; matrix products, arithmetic and copies ran while one was open for 0% -> 0% of each run, Pallas kernels for 0% -> 0%
where the time goes in v1:
time: 114 us; the launch traced here: 113 us
  blocking collectives  30.2 us (26%)
  Pallas kernels  28.8 us (25%)
  starting transfers between devices  25.2 us (22%)
  waiting for transfers between devices  24.2 us (21%)
  local copies, waits for them, and re-layouts  3.23 us (3%)
  between operations  1.35 us (1%)
    all_to_all x1, blocking collectives, everyone(): return lax.all_to_all(copies, axis, split_axis=0, concat_axis=0, tiled=True)  30.2 us
    pallas_call x1, Pallas kernels, factors_of(): pl.pallas_call(functools.partial(factor_kernel, scale), out_shape=[jax.Sh...  17.4 us
    ppermute x2, starting transfers between devices, swapped(): return lax.ppermute(value, 'core', [(0, 1), (1, 0)])  13.9 us
    all_to_all x1, waiting for transfers between devices, everyone(): return lax.all_to_all(copies, axis, split_axis=0, concat_axis=0, tiled=True)  12.2 us
    all_to_all x1, waiting for transfers between devices, summed(): lax.all_to_all(tiles, DEV, split_axis=0, concat_axis=0, tiled=True)  10.4 us
    all_to_all x1, starting transfers between devices, summed(): lax.all_to_all(tiles, DEV, split_axis=0, concat_axis=0, tiled=True)  7.57 us
    pallas_call x1, Pallas kernels, applied(): pl.pallas_call(apply_kernel, grid=(capacity // height,), out_shape=jax.Sh...  6.04 us
    pallas_call x1, Pallas kernels, gram_of(): pl.pallas_call(gram_kernel, out_shape=jax.ShapeDtypeStruct((len(upper_blo...  5.34 us
  transfers between devices with their start and end apart: 4, of which 4 were waited for; matrix products, arithmetic and copies ran while one was open for 0% of the time, Pallas kernels for 0%

profile of v1, /device:TPU:1, one launch (start us, length us, event | category | flops | bytes accessed | tf_op | source)
XLA Modules:
  0.0 113.0 jit_solution(10296631399051844441)
XLA Ops:
  1.3 5.3 %gram.1 = f32[1280,128]{1,0:T(8,128)} custom-call(s32[1]{0:T(128)S(6)} %copy.4.count_ref, f32[1024,512]{1,0:T(8,128)} %rows_ref.3), custom_call_target="tpu_custom_call" | custom-call | tf_op jit(solution)/shard_map/gram/pallas_call | solution.py:47
  6.6 7.6 %all-to-all-start = ((f32[16,80,128]{2,1,0:T(8,128)}), f32[16,80,128]{2,1,0:T(8,128)S(1)}, u32[]{:S(2)}, u32[]{:S(2)}) async-start(f32[16,80,128]{2,1,0:T(8,128)} %bitcast.6), calls=%async_computation | async-start | bytes 1310720 | tf_op jit(solution)/shard_map/all_to_all | solution.py:204
  14.2 10.4 %all-to-all-done = f32[16,80,128]{2,1,0:T(8,128)S(1)} async-done(((f32[16,80,128]{2,1,0:T(8,128)}), f32[16,80,128]{2,1,0:T(8,128)S(1)}, u32[]{:S(2)}, u32[]{:S(2)}) %all-to-all-start) | async-done | bytes 655392 | tf_op jit(solution)/shard_map/all_to_all | solution.py:204
  24.7 5.4 %collective-permute-start = (f32[40,128]{1,0:T(8,128)S(1)}, f32[40,128]{1,0:T(8,128)S(1)}, u32[]{:S(2)}, u32[]{:S(2)}) collective-permute-start(f32[40,128]{1,0:T(8,128)S(1)} %constant_dynamic-slice_fusion.1), channel_id=1, source_target_pairs={{0,16},{16,0},{1,17},{17,1},{2,18},{18,2},{3,19},{19,3},{4,20},{20... | collective-permute-start | bytes 61448 | tf_op jit(solution)/shard_map/ppermute | solution.py:198
  30.1 0.8 collective-permute-done
  31.0 30.2 %all_to_all.15 = f32[16,40,128]{2,1,0:T(8,128)S(1)} all-to-all(f32[16,40,128]{2,1,0:T(8,128)S(1)} %broadcast_in_dim.6), channel_id=1, replica_groups=mesh['z'=16,'core'=2,'y'=4,'x'=4] {'z'}, dimensions={0} | all-to-all | bytes 655360 | tf_op jit(solution)/shard_map/all_to_all | solution.py:194
  61.2 8.4 %collective-permute-start.1 = (f32[40,128]{1,0:T(8,128)S(1)}, f32[40,128]{1,0:T(8,128)S(1)}, u32[]{:S(2)}, u32[]{:S(2)}) collective-permute-start(f32[40,128]{1,0:T(8,128)S(1)} %reduce_sum.19), channel_id=1, source_target_pairs={{0,16},{16,0},{1,17},{17,1},{2,18},{18,2},{3,19},{19,3},{4,20},{20... | collective-permute-start | bytes 61448 | tf_op jit(solution)/shard_map/ppermute | solution.py:198
  69.6 0.8 collective-permute-done.1
  70.4 0.9 broadcast_in_dim.7
  71.3 3.8 %all-to-all-start.2 = ((f32[16,80,128]{2,1,0:T(8,128)}), f32[16,80,128]{2,1,0:T(8,128)S(1)}, u32[]{:S(2)}, u32[]{:S(2)}) async-start(f32[16,80,128]{2,1,0:T(8,128)} %broadcast_in_dim.7), calls=%async_computation.2 | async-start | bytes 1310720 | tf_op jit(solution)/shard_map/all_to_all | solution.py:194
  75.1 12.2 %all-to-all-done.2 = f32[16,80,128]{2,1,0:T(8,128)S(1)} async-done(((f32[16,80,128]{2,1,0:T(8,128)}), f32[16,80,128]{2,1,0:T(8,128)S(1)}, u32[]{:S(2)}, u32[]{:S(2)}) %all-to-all-start.2) | async-done | bytes 655392 | tf_op jit(solution)/shard_map/all_to_all | solution.py:194
  87.3 0.0 copy-start
  87.3 0.8 copy-done
  88.1 17.4 %factor.1 = (f32[512,512]{1,0:T(8,128)}, f32[512,512]{1,0:T(8,128)}) custom-call(f32[1280,128]{1,0:T(8,128)} %bitcast.5), custom_call_target="tpu_custom_call" | custom-call | tf_op jit(solution)/shard_map/factor/pallas_call | solution.py:151
  105.5 6.0 %apply.1 = f32[1024,512]{1,0:T(8,128)} custom-call(s32[1]{0:T(128)S(6)} %copy.4.count_ref, f32[1024,512]{1,0:T(8,128)} %rows_ref.3, f32[512,512]{1,0:T(8,128)} %get-tuple-element.4.inverse_ref), custom_call_target="tpu_custom_call" | custom-call | tf_op jit(solution)/shard_map/apply/pallas_call | solution.py:178
  111.6 1.5 %constant_dynamic-slice_fusion = f32[32,512]{1,0:T(8,128)} fusion(f32[512,512]{1,0:T(8,128)} %get-tuple-element.5, s32[]{:T(128)S(6)} %select_n.26), kind=kLoop, calls=%fused_computation.2 | loop fusion | bytes 131076 | tf_op jit(solution)/shard_map/dynamic_slice | solution.py:222
  (6 shorter events, 0.1 us)
Async XLA Ops:
  6.6 18.0 %all-to-all-start = ((f32[16,80,128]{2,1,0:T(8,128)}), f32[16,80,128]{2,1,0:T(8,128)S(1)}, u32[]{:S(2)}, u32[]{:S(2)}) async-start(f32[16,80,128]{2,1,0:T(8,128)} %bitcast.6), calls=%async_computation | async-start | bytes 1310720 | tf_op jit(solution)/shard_map/all_to_all | solution.py:204
  24.7 6.3 %collective-permute-start = (f32[40,128]{1,0:T(8,128)S(1)}, f32[40,128]{1,0:T(8,128)S(1)}, u32[]{:S(2)}, u32[]{:S(2)}) collective-permute-start(f32[40,128]{1,0:T(8,128)S(1)} %constant_dynamic-slice_fusion.1), channel_id=1, source_target_pairs={{0,16},{16,0},{1,17},{17,1},{2,18},{18,2},{3,19},{19,3},{4,20},{20... | collective-permute-start | bytes 61448 | tf_op jit(solution)/shard_map/ppermute | solution.py:198
  61.2 9.3 %collective-permute-start.1 = (f32[40,128]{1,0:T(8,128)S(1)}, f32[40,128]{1,0:T(8,128)S(1)}, u32[]{:S(2)}, u32[]{:S(2)}) collective-permute-start(f32[40,128]{1,0:T(8,128)S(1)} %reduce_sum.19), channel_id=1, source_target_pairs={{0,16},{16,0},{1,17},{17,1},{2,18},{18,2},{3,19},{19,3},{4,20},{20... | collective-permute-start | bytes 61448 | tf_op jit(solution)/shard_map/ppermute | solution.py:198
  71.3 16.0 %all-to-all-start.2 = ((f32[16,80,128]{2,1,0:T(8,128)}), f32[16,80,128]{2,1,0:T(8,128)S(1)}, u32[]{:S(2)}, u32[]{:S(2)}) async-start(f32[16,80,128]{2,1,0:T(8,128)} %broadcast_in_dim.7), calls=%async_computation.2 | async-start | bytes 1310720 | tf_op jit(solution)/shard_map/all_to_all | solution.py:194
  87.3 0.8 copy-start

commit v2 on v1

--- a/solution.py
+++ b/solution.py
@@ -13,10 +13,15 @@
 B = 128
 NB = 32
 SUB = 8
+CHUNKS = 4
+ROOM = 24 * 1024 * 1024
+MOST = 65_600_000
 DEV = ("y", "x")
-ALL = ("z", "core", "y", "x")
+ALL = ("z_high", "z_low", "core", "y", "x")
+PLANE = ("core", "y", "x")
 HIGH = lax.Precision.HIGHEST
 WHOLE = pl.BlockSpec(memory_space=pltpu.VMEM)
+FAR = pl.BlockSpec(memory_space=pltpu.HBM)
 
 
 def dot(left, right, dims=((1,), (0,))):
@@ -30,25 +35,63 @@
     return [(i, j) for i in range(count) for j in range(i, count)]
 
 
-def gram_kernel(count_ref, rows_ref, packed_ref):
-    capacity, order = rows_ref.shape
-    row = lax.broadcasted_iota(jnp.int32, (capacity, order), 0)
-    live = jnp.where(row < count_ref[0], rows_ref[...], 0.0)
-    at = 0
-    for i in range(order // B):
-        wide = dot(live[:, i * B : (i + 1) * B], live[:, i * B :], ((0,), (0,)))
-        for j in range(order // B - i):
-            packed_ref[at : at + B, :] = wide[:, j * B : (j + 1) * B]
-            at += B
+def halves(value):
+    top = value.astype(jnp.bfloat16)
+    return top, (value - top.astype(jnp.float32)).astype(jnp.bfloat16)
+
+
+def narrow_dot(left, right, dims=((1,), (0,))):
+    return lax.dot_general(left, right, (dims, ((), ())), preferred_element_type=jnp.float32)
+
+
+def gram_kernel(count_ref, rows_ref, packed_ref, rows, sems):
+    capacity, order = rows.shape
+    height = capacity // CHUNKS
+    wide = order // 2
+    copies = [
+        pltpu.make_async_copy(
+            rows_ref.at[pl.ds(c * height, height)],
+            rows.at[pl.ds(c * height, height)],
+            sems.at[c],
+        )
+        for c in range(CHUNKS)
+    ]
+    for copy in copies:
+        copy.start()
+    row = lax.broadcasted_iota(jnp.int32, (height, order), 0)
+    totals = None
+    for c in range(CHUNKS):
+        copies[c].wait()
+        live = jnp.where(
+            row < count_ref[0] - c * height, rows[c * height : (c + 1) * height, :], 0.0
+        )
+        top, low = halves(live)
+        top_t, low_t = halves(live.T)
+        terms = []
+        for lhs_rows, columns in ((wide, slice(0, wide)), (order, slice(wide, order))):
+            term = narrow_dot(top_t[:lhs_rows], top[:, columns])
+            term += narrow_dot(low_t[:lhs_rows], top[:, columns])
+            term += narrow_dot(top_t[:lhs_rows], low[:, columns])
+            term += narrow_dot(low_t[:lhs_rows], low[:, columns])
+            terms.append(term)
+        totals = terms if totals is None else [t + u for t, u in zip(totals, terms)]
+    for p, (i, j) in enumerate(upper_blocks(order)):
+        side, inner = divmod(j * B, wide)
+        packed_ref[p * B : (p + 1) * B, :] = totals[side][i * B : (i + 1) * B, inner : inner + B]
 
 
 def gram_of(rows_in, count):
-    order = rows_in.shape[1]
+    capacity, order = rows_in.shape
     return pl.pallas_call(
         gram_kernel,
         out_shape=jax.ShapeDtypeStruct((len(upper_blocks(order)) * B, B), jnp.float32),
-        in_specs=[pl.BlockSpec(memory_space=pltpu.SMEM), WHOLE],
+        in_specs=[pl.BlockSpec(memory_space=pltpu.SMEM), FAR],
         out_specs=WHOLE,
+        scratch_shapes=[
+            pltpu.VMEM((capacity, order), jnp.float32),
+            pltpu.SemaphoreType.DMA((CHUNKS,)),
+        ],
+        compiler_params=pltpu.CompilerParams(vmem_limit_bytes=MOST),
         name="gram",
     )(count, rows_in)
 
@@ -116,7 +159,7 @@
     return jnp.concatenate(upper), jnp.concatenate(inverse)
 
 
-def factor_kernel(scale, packed_ref, upper_ref, inverse_ref, work):
+def factor(scale, packed_ref, upper_ref, inverse_ref, work):
     order = work.shape[0]
     for p, (i, j) in enumerate(upper_blocks(order)):
         work[i * B : (i + 1) * B, j * B : (j + 1) * B] = (
@@ -147,69 +190,79 @@
             work[hi:, hi:] = work[hi:, hi:] - change[:, hi:]
 
 
-def factors_of(packed, order, scale):
+def solve_kernel(
+    scale, scalars_ref, packed_ref, rows, out_ref, share_ref,
+    work, upper, inverse, result, out_sems,
+):
+    capacity, order = rows.shape
+    height = capacity // CHUNKS
+    half = order // 2
+    factor(scale, packed_ref, upper, inverse, work)
+    share = share_ref.shape[0]
+    at = pl.multiple_of(scalars_ref[1] * share, share)
+    share_ref[...] = upper[pl.ds(at, share), :]
+    top, low = halves(inverse[...])
+    row = lax.broadcasted_iota(jnp.int32, (height, order), 0)
+    stores = []
+    for c in range(CHUNKS):
+        span = slice(c * height, (c + 1) * height)
+        live = jnp.where(row < scalars_ref[0] - c * height, rows[span, :], 0.0)
+        live_top, live_low = halves(live)
+        for k in range(2):
+            lo, hi = k * half, (k + 1) * half
+            value = narrow_dot(live_top[:, :hi], top[lo:hi, :hi], ((1,), (1,)))
+            value += narrow_dot(live_low[:, :hi], top[lo:hi, :hi], ((1,), (1,)))
+            value += narrow_dot(live_top[:, :hi], low[lo:hi, :hi], ((1,), (1,)))
+            result[span, lo:hi] = value
+        store = pltpu.make_async_copy(
+            result.at[pl.ds(c * height, height)],
+            out_ref.at[pl.ds(c * height, height)],
+            out_sems.at[c],
+        )
+        store.start()
+        stores.append(store)
+    for store in stores:
+        store.wait()
+
+
+def solved(packed, rows_in, count, index, members, scale):
+    capacity, order = rows_in.shape
+    square = pltpu.VMEM((order, order), jnp.float32)
+    tall = pltpu.VMEM((capacity, order), jnp.float32)
     return pl.pallas_call(
-        functools.partial(factor_kernel, scale),
-        out_shape=[jax.ShapeDtypeStruct((order, order), jnp.float32)] * 2,
-        in_specs=[WHOLE],
-        out_specs=[WHOLE] * 2,
-        scratch_shapes=[pltpu.VMEM((order, order), jnp.float32)],
-        name="factor",
-    )(packed)
-
-
-def apply_kernel(count_ref, rows_ref, inverse_ref, out_ref):
-    height, order = rows_ref.shape
-    row = lax.broadcasted_iota(jnp.int32, (height, order), 0)
-    start = pl.program_id(0) * height
-    live = jnp.where(row + start < count_ref[0], rows_ref[...], 0.0)
-    half = order // 2
-    for k in range(2):
-        hi = (k + 1) * half
-        out_ref[:, k * half : hi] = dot(
-            live[:, :hi], inverse_ref[k * half : hi, :hi], ((1,), (1,))
-        )
-
-
-def applied(rows_in, count, inverse):
-    capacity, order = rows_in.shape
-    height = capacity // 4
-    tile = pl.BlockSpec((height, order), lambda i: (i, 0))
-    return pl.pallas_call(
-        apply_kernel,
-        grid=(capacity // height,),
-        out_shape=jax.ShapeDtypeStruct(rows_in.shape, jnp.float32),
-        in_specs=[
-            pl.BlockSpec(memory_space=pltpu.SMEM),
-            tile,
-            pl.BlockSpec((order, order), lambda i: (0, 0)),
+        functools.partial(solve_kernel, scale),
+        out_shape=[
+            jax.ShapeDtypeStruct(rows_in.shape, jnp.float32),
+            jax.ShapeDtypeStruct((order // members, order), jnp.float32),
         ],
-        out_specs=tile,
-        name="apply",
-    )(count, rows_in, inverse)
+        in_specs=[pl.BlockSpec(memory_space=pltpu.SMEM), WHOLE, WHOLE],
+        out_specs=[FAR, WHOLE],
+        scratch_shapes=[
+            square,
+            square,
+            square,
+            tall,
+            pltpu.SemaphoreType.DMA((CHUNKS,)),
+        ],
+        compiler_params=pltpu.CompilerParams(vmem_limit_bytes=ROOM),
+        name="solve",
+    )(jnp.stack([count[0], index]), packed, rows_in)
+
+
+def exchanged(tiles, axis):
+    return lax.all_to_all(tiles, axis, split_axis=0, concat_axis=0, tiled=True)
 
 
 def everyone(value, axis):
-    copies = jnp.broadcast_to(value, (lax.axis_size(axis), *value.shape))
-    return lax.all_to_all(copies, axis, split_axis=0, concat_axis=0, tiled=True)
-
-
-def swapped(value):
-    return lax.ppermute(value, "core", [(0, 1), (1, 0)])
+    return exchanged(jnp.broadcast_to(value, (lax.axis_size(axis), *value.shape)), axis)
 
 
 def summed(packed):
-    members = lax.axis_size(DEV)
-    tiles = packed.reshape(members, -1, B)
-    own = lax.all_to_all(tiles, DEV, split_axis=0, concat_axis=0, tiled=True).sum(axis=0)
-    core = lax.axis_index("core")
-    half = own.shape[0] // 2
-    mine = lax.dynamic_slice_in_dim(own, core * half, half, 0)
-    other = lax.dynamic_slice_in_dim(own, (1 - core) * half, half, 0)
-    part = everyone(mine + swapped(other), "z").sum(axis=0)
-    back = swapped(part)
-    own = jnp.where(core == 0, jnp.stack([part, back]), jnp.stack([back, part]))
-    return everyone(own.reshape(-1, B), DEV).reshape(-1, B)
+    tiles = packed.reshape(lax.axis_size(PLANE), -1, B)
+    own = exchanged(tiles, PLANE).sum(axis=0)
+    own = everyone(own, "z_low").sum(axis=0)
+    own = everyone(own, "z_high").sum(axis=0)
+    return everyone(own, PLANE).reshape(-1, B)
 
 
 def shards(sketch, row_counts):
@@ -217,14 +270,11 @@
     members = lax.axis_size(DEV)
     row_total = lax.axis_size(ALL) * HOLD * (capacity // SLOTS)
     packed = summed(gram_of(sketch, row_counts))
-    upper, inverse = factors_of(packed, order, 1.0 / row_total)
-    share = order // members
-    r_rows = lax.dynamic_slice_in_dim(upper, lax.axis_index(DEV) * share, share, 0)
-    return (applied(sketch, row_counts, inverse), r_rows)
+    return solved(packed, sketch, row_counts, lax.axis_index(DEV), members, 1.0 / row_total)
 
 
 def solution(mesh):
-    finer = Mesh(mesh.devices.reshape(16, 2, 4, 4), ALL)
+    finer = Mesh(mesh.devices.reshape(4, 4, 2, 4, 4), ALL)
     return jax.shard_map(
         shards,
         mesh=finer,

time: 114 us -> 101 us (0.89)
  blocking collectives: 30.2 us -> 54.8 us
  starting transfers between devices: 25.2 us -> 7.95 us
  waiting for transfers between devices: 24.2 us -> 12 us
  Pallas kernels: 28.8 us -> 23.8 us
  local copies, waits for them, and re-layouts: 3.23 us -> 0.9 us
    all_to_all x1 -> x3, blocking collectives: 30.2 us -> 54.8 us  [exchanged(): return lax.all_to_all(tiles, axis, split_axis=0, concat_axis=0, tiled=True)]
    ppermute x2 -> x0, starting transfers between devices: 13.9 us -> none  [swapped(): return lax.ppermute(value, 'core', [(0, 1), (1, 0)])]
    all_to_all x2 -> x1, waiting for transfers between devices: 22.6 us -> 12 us  [exchanged(): return lax.all_to_all(tiles, axis, split_axis=0, concat_axis=0, tiled=True)]
    pallas_call x2 -> x1, Pallas kernels: 23.5 us -> 18.7 us  [solved(): pl.pallas_call(functools.partial(solve_kernel, scale), out_shape=[jax.Sha...]
    all_to_all x2 -> x1, starting transfers between devices: 11.3 us -> 7.95 us  [exchanged(): return lax.all_to_all(tiles, axis, split_axis=0, concat_axis=0, tiled=True)]
    ppermute x2 -> x0, waiting for transfers between devices: 1.64 us -> none  [swapped(): return lax.ppermute(value, 'core', [(0, 1), (1, 0)])]
    dynamic_slice x2 -> x0, local copies, waits for them, and re-layouts: 1.48 us -> none  [the longest x1 1.47 us: shards(): lax.dynamic_slice_in_dim(upper, lax.axis_index(DEV) * share, share, 0)]
  transfers between devices with their start and end apart: 4 -> 1, of which waited for: 4 -> 1; matrix products, arithmetic and copies ran while one was open for 0% -> 0% of each run, Pallas kernels for 0% -> 0%
where the time goes in v2:
time: 101 us
  blocking collectives  54.8 us (54%)
  Pallas kernels  23.8 us (24%)
  waiting for transfers between devices  12 us (12%)
  starting transfers between devices  7.95 us (8%)
  between operations  1.49 us (1%)
    all_to_all x3, blocking collectives, exchanged(): return lax.all_to_all(tiles, axis, split_axis=0, concat_axis=0, tiled=True)  54.8 us
    pallas_call x1, Pallas kernels, solved(): pl.pallas_call(functools.partial(solve_kernel, scale), out_shape=[jax.Sha...  18.7 us
    all_to_all x1, waiting for transfers between devices, exchanged(): return lax.all_to_all(tiles, axis, split_axis=0, concat_axis=0, tiled=True)  12 us
    all_to_all x1, starting transfers between devices, exchanged(): return lax.all_to_all(tiles, axis, split_axis=0, concat_axis=0, tiled=True)  7.95 us
    pallas_call x1, Pallas kernels, gram_of(): pl.pallas_call(gram_kernel, out_shape=jax.ShapeDtypeStruct((len(upper_blo...  5.03 us
  transfers between devices with their start and end apart: 1, of which 1 were waited for; matrix products, arithmetic and copies ran while one was open for 0% of the time, Pallas kernels for 0%

profile of v2, /device:TPU:1, one launch (start us, length us, event | category | flops | bytes accessed | tf_op | source)
XLA Modules:
  0.0 101.1 jit_solution(2859078753245930940)
XLA Ops:
  1.3 5.0 %gram.1 = f32[1280,128]{1,0:T(8,128)} custom-call(s32[1]{0:T(128)S(6)} %copy.4.count_ref, f32[1024,512]{1,0:T(8,128)} %rows.1), custom_call_target="tpu_custom_call" | custom-call | tf_op jit(solution)/shard_map/gram/pallas_call | solution.py:85
  6.3 0.0 copy-start
  6.3 22.9 %all_to_all.20 = f32[32,40,128]{2,1,0:T(8,128)S(1)} all-to-all(f32[32,40,128]{2,1,0:T(8,128)} %bitcast.4), channel_id=1, replica_groups=mesh['z_high'=4,'z_low'=4,'core'=2,'y'=4,'x'=4] {'core','y','x'}, dimensions={0} | all-to-all | bytes 1310720 | tf_op jit(solution)/shard_map/all_to_all | solution.py:253
  29.3 0.1 reduce_sum.27
  29.3 8.1 %all_to_all.21 = f32[4,40,128]{2,1,0:T(8,128)S(1)} all-to-all(f32[4,40,128]{2,1,0:T(8,128)S(1)} %broadcast_in_dim.9), channel_id=1, replica_groups=mesh['z_high'=4,'z_low'=4,'core'=2,'y'=4,'x'=4] {'z_low'}, dimensions={0} | all-to-all | bytes 163840 | tf_op jit(solution)/shard_map/all_to_all | solution.py:253
  37.5 23.7 %all_to_all.22 = f32[4,40,128]{2,1,0:T(8,128)S(1)} all-to-all(f32[4,40,128]{2,1,0:T(8,128)S(1)} %broadcast_in_dim.10), channel_id=1, replica_groups=mesh['z_high'=4,'z_low'=4,'core'=2,'y'=4,'x'=4] {'z_high'}, dimensions={0} | all-to-all | bytes 163840 | tf_op jit(solution)/shard_map/all_to_all | solution.py:253
  61.2 0.9 broadcast_in_dim.11
  62.1 8.0 %all-to-all-start.3 = ((f32[32,40,128]{2,1,0:T(8,128)}), f32[32,40,128]{2,1,0:T(8,128)S(1)}, u32[]{:S(2)}, u32[]{:S(2)}) async-start(f32[32,40,128]{2,1,0:T(8,128)} %broadcast_in_dim.11), calls=%async_computation.3 | async-start | bytes 1310720 | tf_op jit(solution)/shard_map/all_to_all | solution.py:253
  70.0 0.1 pad_add_fusion.scalars_ref
  70.1 12.0 %all-to-all-done.3 = f32[32,40,128]{2,1,0:T(8,128)S(1)} async-done(((f32[32,40,128]{2,1,0:T(8,128)}), f32[32,40,128]{2,1,0:T(8,128)S(1)}, u32[]{:S(2)}, u32[]{:S(2)}) %all-to-all-start.3) | async-done | bytes 655392 | tf_op jit(solution)/shard_map/all_to_all | solution.py:253
  82.2 0.0 copy-done
  82.2 18.7 %solve.1 = (f32[1024,512]{1,0:T(8,128)}, f32[32,512]{1,0:T(8,128)}) custom-call(s32[2]{0:T(128)S(1)} %pad_add_fusion.scalars_ref, f32[1280,128]{1,0:T(8,128)S(1)} %bitcast.3, f32[1024,512]{1,0:T(8,128)S(1)} %copy-done), custom_call_target="tpu_custom_call" | custom-call | tf_op jit(solution)/shard_map/solve/pallas_call | solution.py:232
  (4 shorter events, 0.0 us)
Async XLA Ops:
  6.3 75.8 %copy-start = (f32[1024,512]{1,0:T(8,128)S(1)}, f32[1024,512]{1,0:T(8,128)}, u32[]{:S(2)}) copy-start(f32[1024,512]{1,0:T(8,128)} %rows.1) | copy-start | bytes 6291460
  62.1 20.1 %all-to-all-start.3 = ((f32[32,40,128]{2,1,0:T(8,128)}), f32[32,40,128]{2,1,0:T(8,128)S(1)}, u32[]{:S(2)}, u32[]{:S(2)}) async-start(f32[32,40,128]{2,1,0:T(8,128)} %broadcast_in_dim.11), calls=%async_computation.3 | async-start | bytes 1310720 | tf_op jit(solution)/shard_map/all_to_all | solution.py:253

commit v3 on v2

v3 whole, which is shorter than its diff:
```python
import functools

import jax
import jax.numpy as jnp
from jax import lax
from jax.experimental import pallas as pl
from jax.experimental.pallas import tpu as pltpu
from jax.sharding import Mesh
from jax.sharding import PartitionSpec as P

SLOTS = 16
HOLD = 4
B = 128
NB = 32
SUB = 8
CHUNKS = 4
ROOM = 24 * 1024 * 1024
LEFT, RIGHT = (2, 1, 0, 1, 0, 0), (0, 1, 2, 0, 1, 0)
LEFT_WIDE, RIGHT_WIDE = (2, 1, *LEFT), (1, 2, *RIGHT)
DEV = ("y", "x")
ALL = ("z_high", "z_low", "core", "y", "x")
PLANE = ("core", "y", "x")
HIGH = lax.Precision.HIGHEST
WHOLE = pl.BlockSpec(memory_space=pltpu.VMEM)
FAR = pl.BlockSpec(memory_space=pltpu.HBM)


def dot(left, right, dims=((1,), (0,))):
    return lax.dot_general(
        left, right, (dims, ((), ())), precision=HIGH, preferred_element_type=jnp.float32
    )


def upper_blocks(order):
    count = order // B
    return [(i, j) for i in range(count) for j in range(i, count)]


def halves(value):
    top = value.astype(jnp.bfloat16)
    return top, (value - top.astype(jnp.float32)).astype(jnp.bfloat16)


def narrow_dot(left, right, dims=((1,), (0,))):
    return lax.dot_general(left, right, (dims, ((), ())), preferred_element_type=jnp.float32)


def gram_kernel(count_ref, rows, packed_ref, left_sum, right_sum):
    capacity, order = rows.shape
    height = capacity // CHUNKS
    wide = order // 2

    left_sum[...] = jnp.zeros_like(left_sum)
    right_sum[...] = jnp.zeros_like(right_sum)
    row = lax.broadcasted_iota(jnp.int32, (height, order), 0)

    @pl.loop(0, CHUNKS)
    def _(c):
        held = rows[pl.ds(pl.multiple_of(c * height, height), height), :]
        live = jnp.where(row < count_ref[0] - c * height, held, 0.0)
        top, low = halves(live)
        top_t, low_t = halves(live.T)
        for total, side in ((left_sum, slice(0, wide)), (right_sum, slice(wide, order))):
            tall = total.shape[0]
            term = narrow_dot(top_t[:tall], top[:, side])
            term += narrow_dot(low_t[:tall], top[:, side])
            term += narrow_dot(top_t[:tall], low[:, side])
            term += narrow_dot(low_t[:tall], low[:, side])
            total[...] += term

    for p, (i, j) in enumerate(upper_blocks(order)):
        side, inner = divmod(j * B, wide)
        total = (left_sum, right_sum)[side]
        packed_ref[p * B : (p + 1) * B, :] = total[i * B : (i + 1) * B, inner : inner + B]


def gram_of(rows_in, count):
    capacity, order = rows_in.shape
    return pl.pallas_call(
        gram_kernel,
        out_shape=jax.ShapeDtypeStruct((len(upper_blocks(order)) * B, B), jnp.float32),
        in_specs=[pl.BlockSpec(memory_space=pltpu.SMEM), WHOLE],
        out_specs=WHOLE,
        scratch_shapes=[
            pltpu.VMEM((order // 2, order // 2), jnp.float32),
            pltpu.VMEM((order, order // 2), jnp.float32),
        ],
        compiler_params=pltpu.CompilerParams(vmem_limit_bytes=ROOM),
        name="gram",
    )(count, rows_in)


def spread(row):
    return jnp.broadcast_to(row, (SUB, row.shape[1]))


def thirds(value):
    top = value.astype(jnp.bfloat16)
    rest = value - top.astype(jnp.float32)
    middle = rest.astype(jnp.bfloat16)
    return top, middle, (rest - middle.astype(jnp.float32)).astype(jnp.bfloat16)


def stacked(value, order, axis):
    parts = thirds(value)
    return jnp.concatenate([parts[k] for k in order], axis=axis)


def exact_dot(left, right):
    return narrow_dot(stacked(left, LEFT, 1), stacked(right, RIGHT, 0))


def eliminate(strip, at):
    groups = NB // SUB
    lane = lax.broadcasted_iota(jnp.int32, (SUB, B), 1)
    sub = lax.broadcasted_iota(jnp.int32, (SUB, B), 0)
    rows = [strip[v * SUB : (v + 1) * SUB] for v in range(groups)]
    cols = [
        [
            None
            if v < j // SUB
            else jnp.broadcast_to(rows[v][:, at + j : at + j + 1], (SUB, B))
            for v in range(groups)
        ]
        for j in range(NB)
    ]
    diagonal = (lane >= at) & (lane < at + NB)
    rows = [
        jnp.where(diagonal, (lane == sub + (at + v * SUB)).astype(jnp.float32), rows[v])
        for v in range(groups)
    ]
    done = list(rows)
    for j in range(NB):
        first, r = divmod(j, SUB)
        root = lax.rsqrt(spread(cols[j][first][r : r + 1]))
        scaled = [None if c is None else c * root for c in cols[j]]
        row = spread(rows[first][r : r + 1]) * root
        done[first] = jnp.where(sub == r, row, done[first])
        for l in range(j + 1, NB):
            g, q = divmod(l, SUB)
            factor = spread(scaled[g][q : q + 1])
            for v in range(g, groups):
                cols[l][v] = cols[l][v] - scaled[v] * factor
        for v in range(first, groups):
            rows[v] = rows[v] - scaled[v] * row
        cols[j] = None
    return jnp.concatenate(done)


def factor_block(block):
    strips = [block[b * NB : (b + 1) * NB] for b in range(B // NB)]
    lane = lax.broadcasted_iota(jnp.int32, (NB, B), 1)
    sub = lax.broadcasted_iota(jnp.int32, (NB, B), 0)
    inverse = []
    for b in range(B // NB):
        at = b * NB
        done = eliminate(strips[b], at)
        inverse.append(jnp.where(lane <= sub + at, done, 0.0))
        if at + NB < B:
            across = stacked(done, LEFT_WIDE, 0).T
            down = stacked(done, RIGHT_WIDE, 0)
            hit = (lane >= at) & (lane < at + NB)
            near = narrow_dot(across[at + NB : at + 2 * NB], down)
            strips[b + 1] = jnp.where(hit, 0.0, strips[b + 1]) - near
            if at + 2 * NB < B:
                rest = narrow_dot(across[at + 2 * NB :], down)
                for i in range(b + 2, B // NB):
                    o = (i - b - 2) * NB
                    strips[i] = jnp.where(hit, 0.0, strips[i]) - rest[o : o + NB]
    return jnp.concatenate(inverse)


def factor(scale, packed_ref, upper_ref, top_ref, low_ref, work):
    order = work.shape[0]
    for p, (i, j) in enumerate(upper_blocks(order)):
        work[i * B : (i + 1) * B, j * B : (j + 1) * B] = (
            packed_ref[p * B : (p + 1) * B, :] * scale
        )
    lane = lax.broadcasted_iota(jnp.int32, (B, B), 1)
    sub = lax.broadcasted_iota(jnp.int32, (B, B), 0)
    for s in range(order // B):
        lo, hi = s * B, (s + 1) * B
        here = slice(lo, hi)
        inverse = factor_block(work[here, here])
        across = stacked(inverse, LEFT, 1)
        if hi < order:
            near = slice(hi, hi + B)
            right = narrow_dot(across, stacked(work[here, near], RIGHT, 0))
            work[near, near] = work[near, near] - exact_dot(right.T, right)
            rights = [right]
            if hi + B < order:
                far = narrow_dot(across, stacked(work[here, hi + B :], RIGHT, 0))
                rights += [far[:, c : c + B] for c in range(0, far.shape[1], B)]
            for c, right in enumerate(rights):
                upper_ref[here, hi + c * B : hi + (c + 1) * B] = right
        own = narrow_dot(across, stacked(work[here, here], RIGHT, 0))
        upper_ref[here, here] = jnp.where(lane >= sub, own, 0.0)
        lefts = [inverse]
        if lo:
            left = narrow_dot(across, stacked(work[here, :lo], RIGHT, 0))
            upper_ref[here, :lo] = jnp.zeros((B, lo), jnp.float32)
            lefts = [left, inverse]
        lefts = jnp.concatenate(lefts, axis=1)
        top_ref[here, :hi], low_ref[here, :hi] = halves(lefts)
        if s % 2 == 0 and hi < order:
            top_ref[here, hi : hi + B] = jnp.zeros((B, B), jnp.bfloat16)
            low_ref[here, hi : hi + B] = jnp.zeros((B, B), jnp.bfloat16)
        if hi < order:
            turned = [stacked(right.T, LEFT, 1) for right in rights]
            change = narrow_dot(jnp.concatenate(turned), stacked(lefts, RIGHT, 0))
            if lo:
                work[hi:, :lo] = work[hi:, :lo] - change[:, :lo]
            work[hi:, here] = -change[:, lo:]
            for c in range(1, len(rights)):
                span = slice(hi + c * B, hi + (c + 1) * B)
                change = narrow_dot(
                    jnp.concatenate(turned[: c + 1]), stacked(rights[c], RIGHT, 0)
                )
                work[hi : hi + (c + 1) * B, span] = work[hi : hi + (c + 1) * B, span] - change


def solve_kernel(
    scale, scalars_ref, packed_ref, rows_ref, out_ref, share_ref,
    work, upper, top, low, result, sems,
):
    capacity, order = rows_ref.shape
    height = capacity // CHUNKS
    half = order // 2
    factor(scale, packed_ref, upper, top, low, work)
    share = share_ref.shape[0]
    share_ref[...] = upper[pl.ds(pl.multiple_of(scalars_ref[1] * share, share), share), :]
    row = lax.broadcasted_iota(jnp.int32, (height, order), 0)

    def store(c):
        span = pl.ds(pl.multiple_of(c * height, height), height)
        return pltpu.make_async_copy(result.at[span], out_ref.at[span], sems.at[c])

    @pl.loop(0, CHUNKS)
    def _(c):
        span = pl.ds(pl.multiple_of(c * height, height), height)
        live = jnp.where(row < scalars_ref[0] - c * height, rows_ref[span, :], 0.0)
        live_top, live_low = halves(live)
        for k in range(2):
            lo, hi = k * half, (k + 1) * half
            value = narrow_dot(live_top[:, :hi], top[lo:hi, :hi], ((1,), (1,)))
            value += narrow_dot(live_low[:, :hi], top[lo:hi, :hi], ((1,), (1,)))
            value += narrow_dot(live_top[:, :hi], low[lo:hi, :hi], ((1,), (1,)))
            result[span, lo:hi] = value
        store(c).start()

    for c in range(CHUNKS):
        store(c).wait()


def solved(packed, rows_in, scalars, members, scale):
    capacity, order = rows_in.shape
    square = pltpu.VMEM((order, order), jnp.float32)
    tall = pltpu.VMEM((capacity, order), jnp.float32)
    return pl.pallas_call(
        functools.partial(solve_kernel, scale),
        out_shape=[
            jax.ShapeDtypeStruct(rows_in.shape, jnp.float32),
            jax.ShapeDtypeStruct((order // members, order), jnp.float32),
        ],
        in_specs=[pl.BlockSpec(memory_space=pltpu.SMEM), WHOLE, WHOLE],
        out_specs=[FAR, WHOLE],
        scratch_shapes=[
            square,
            square,
            pltpu.VMEM((order, order), jnp.bfloat16),
            pltpu.VMEM((order, order), jnp.bfloat16),
            tall,
            pltpu.SemaphoreType.DMA((CHUNKS,)),
        ],
        compiler_params=pltpu.CompilerParams(vmem_limit_bytes=ROOM),
        name="solve",
    )(scalars, packed, rows_in)


def exchanged(tiles, axis):
    return lax.all_to_all(tiles, axis, split_axis=0, concat_axis=0, tiled=True)


def everyone(value, axis):
    return exchanged(jnp.broadcast_to(value, (lax.axis_size(axis), *value.shape)), axis)


def summed(packed):
    tiles = packed.reshape(lax.axis_size(PLANE), -1, B)
    own = exchanged(tiles, PLANE).sum(axis=0)
    own = everyone(own, "z_low").sum(axis=0)
    own = everyone(own, "z_high").sum(axis=0)
    return everyone(own, PLANE).reshape(-1, B)


def shards(sketch, row_counts):
    capacity, order = sketch.shape
    members = lax.axis_size(DEV)
    row_total = lax.axis_size(ALL) * HOLD * (capacity // SLOTS)
    scalars = jnp.stack([row_counts[0], lax.axis_index(DEV)])
    packed = summed(gram_of(sketch, scalars))
    return solved(packed, sketch, scalars, members, 1.0 / row_total)


def solution(mesh):
    finer = Mesh(mesh.devices.reshape(4, 4, 2, 4, 4), ALL)
    return jax.shard_map(
        shards,
        mesh=finer,
        in_specs=(P(ALL, None), P(ALL)),
        out_specs=(P(ALL, None), P(DEV, None)),
        check_vma=False,
    )
```

time: 101 us -> 98.1 us (0.971)
  blocking collectives: 54.8 us -> 74.1 us
  waiting for transfers between devices: 12 us -> 0 us
  starting transfers between devices: 7.95 us -> 0 us
  Pallas kernels: 23.8 us -> 20.6 us
    all_to_all x3 -> x4, blocking collectives: 54.8 us -> 74.1 us  [exchanged(): return lax.all_to_all(tiles, axis, split_axis=0, concat_axis=0, tiled=True)]
    all_to_all x1 -> x0, waiting for transfers between devices: 12 us -> none  [exchanged(): return lax.all_to_all(tiles, axis, split_axis=0, concat_axis=0, tiled=True)]
    all_to_all x1 -> x0, starting transfers between devices: 7.95 us -> none  [exchanged(): return lax.all_to_all(tiles, axis, split_axis=0, concat_axis=0, tiled=True)]
    pallas_call x1, Pallas kernels: 5.03 us -> 3.22 us  [gram_of(): pl.pallas_call(gram_kernel, out_shape=jax.ShapeDtypeStruct((len(upper_blo...]
    unnamed x2 -> x4, local copies, waits for them, and re-layouts: 0.01 us -> 1.6 us
    pallas_call x1, Pallas kernels: 18.7 us -> 17.4 us  [solved(): pl.pallas_call(functools.partial(solve_kernel, scale), out_shape=[jax.Sha...]
  transfers between devices with their start and end apart: 1 -> 0, of which waited for: 1 -> 0; matrix products, arithmetic and copies ran while one was open for 0% -> 0% of each run, Pallas kernels for 0% -> 0%
where the time goes in v3:
time: 98.1 us; the launch traced here: 97.8 us
  blocking collectives  74.1 us (76%)
  Pallas kernels  20.6 us (21%)
  local copies, waits for them, and re-layouts  1.66 us (2%)
  between operations  1.32 us (1%)
    all_to_all x4, blocking collectives, exchanged(): return lax.all_to_all(tiles, axis, split_axis=0, concat_axis=0, tiled=True)  74.1 us
    pallas_call x1, Pallas kernels, solved(): pl.pallas_call(functools.partial(solve_kernel, scale), out_shape=[jax.Sha...  17.4 us
    pallas_call x1, Pallas kernels, gram_of(): pl.pallas_call(gram_kernel, out_shape=jax.ShapeDtypeStruct((len(upper_blo...  3.22 us

profile of v3, /device:TPU:1, one launch (start us, length us, event | category | flops | bytes accessed | tf_op | source)
XLA Modules:
  0.0 97.8 jit_solution(6099327214578787894)
XLA Ops:
  1.3 0.1 pad_add_fusion.count_ref.scalars_ref
  1.4 0.0 copy-start
  1.4 1.6 %copy-done = f32[1024,512]{1,0:T(8,128)S(1)} copy-done((f32[1024,512]{1,0:T(8,128)S(1)}, f32[1024,512]{1,0:T(8,128)}, u32[]{:S(2)}) %copy-start) | copy-done | bytes 2097176
  2.9 3.2 %gram.1 = f32[1280,128]{1,0:T(8,128)S(1)} custom-call(s32[2]{0:T(128)S(1)} %pad_add_fusion.count_ref.scalars_ref, f32[1024,512]{1,0:T(8,128)S(1)} %copy-done), custom_call_target="tpu_custom_call" | custom-call | tf_op jit(solution)/shard_map/gram/pallas_call | solution.py:79
  6.2 0.0 copy-start.1
  6.2 22.0 %all_to_all.20 = f32[32,40,128]{2,1,0:T(8,128)S(1)} all-to-all(f32[32,40,128]{2,1,0:T(8,128)S(1)} %bitcast.4), channel_id=1, replica_groups=mesh['z_high'=4,'z_low'=4,'core'=2,'y'=4,'x'=4] {'core','y','x'}, dimensions={0} | all-to-all | bytes 1310720 | tf_op jit(solution)/shard_map/all_to_all | solution.py:281
  28.2 0.1 reduce_sum.27
  28.3 8.8 %all_to_all.21 = f32[4,40,128]{2,1,0:T(8,128)S(1)} all-to-all(f32[4,40,128]{2,1,0:T(8,128)S(1)} %broadcast_in_dim.9), channel_id=1, replica_groups=mesh['z_high'=4,'z_low'=4,'core'=2,'y'=4,'x'=4] {'z_low'}, dimensions={0} | all-to-all | bytes 163840 | tf_op jit(solution)/shard_map/all_to_all | solution.py:281
  37.1 23.7 %all_to_all.22 = f32[4,40,128]{2,1,0:T(8,128)S(1)} all-to-all(f32[4,40,128]{2,1,0:T(8,128)S(1)} %broadcast_in_dim.10), channel_id=1, replica_groups=mesh['z_high'=4,'z_low'=4,'core'=2,'y'=4,'x'=4] {'z_high'}, dimensions={0} | all-to-all | bytes 163840 | tf_op jit(solution)/shard_map/all_to_all | solution.py:281
  60.9 19.5 %all_to_all.23 = f32[32,40,128]{2,1,0:T(8,128)S(1)} all-to-all(f32[32,40,128]{2,1,0:T(8,128)S(1)} %broadcast_in_dim.11), channel_id=1, replica_groups=mesh['z_high'=4,'z_low'=4,'core'=2,'y'=4,'x'=4] {'core','y','x'}, dimensions={0} | all-to-all | bytes 1310720 | tf_op jit(solution)/shard_map/all_to_all | solution.py:281
  80.4 0.0 copy-done.1
  80.5 17.4 %solve.1 = (f32[1024,512]{1,0:T(8,128)}, f32[32,512]{1,0:T(8,128)}) custom-call(s32[2]{0:T(128)S(1)} %pad_add_fusion.count_ref.scalars_ref, f32[1280,128]{1,0:T(8,128)S(1)} %bitcast.3, f32[1024,512]{1,0:T(8,128)S(1)} %copy-done.1), custom_call_target="tpu_custom_call" | custom-call | tf_op jit(solution)/shard_map/solve/pallas_call | solution.py:259
  (5 shorter events, 0.1 us)
Async XLA Ops:
  1.4 1.6 %copy-start = (f32[1024,512]{1,0:T(8,128)S(1)}, f32[1024,512]{1,0:T(8,128)}, u32[]{:S(2)}) copy-start(f32[1024,512]{1,0:T(8,128)} %rows_ref.1) | copy-start | bytes 6291460
  6.2 74.3 %copy-start.1 = (f32[1024,512]{1,0:T(8,128)S(1)}, f32[1024,512]{1,0:T(8,128)}, u32[]{:S(2)}) copy-start(f32[1024,512]{1,0:T(8,128)} %rows_ref.1) | copy-start | bytes 6291460

commit v4 on v3

--- a/solution.py
+++ b/solution.py
@@ -36,6 +36,11 @@
     return [(i, j) for i in range(count) for j in range(i, count)]
 
 
+def packed_rows(order):
+    count = order // B
+    return count * (count - 1) // 2 * B + count // 2 * (B + B // 2)
+
+
 def halves(value):
     top = value.astype(jnp.bfloat16)
     return top, (value - top.astype(jnp.float32)).astype(jnp.bfloat16)
@@ -68,17 +73,33 @@
             term += narrow_dot(low_t[:tall], low[:, side])
             total[...] += term
 
-    for p, (i, j) in enumerate(upper_blocks(order)):
+    def block(i, j):
         side, inner = divmod(j * B, wide)
         total = (left_sum, right_sum)[side]
-        packed_ref[p * B : (p + 1) * B, :] = total[i * B : (i + 1) * B, inner : inner + B]
+        return total[i * B : (i + 1) * B, inner : inner + B]
+
+    at = 0
+    for i, j in upper_blocks(order):
+        if i != j:
+            packed_ref[at : at + B, :] = block(i, j)
+            at += B
+    half = B // 2
+    lane = lax.broadcasted_iota(jnp.int32, (half, B), 1)
+    for i in range(0, order // B, 2):
+        first, second = block(i, i), block(i + 1, i + 1)
+        packed_ref[at : at + half, :] = first[:half]
+        packed_ref[at + half : at + B, :] = second[:half]
+        packed_ref[at + B : at + B + half, :] = jnp.where(
+            lane < half, pltpu.roll(first[half:], half, 1), second[half:]
+        )
+        at += B + half
 
 
 def gram_of(rows_in, count):
     capacity, order = rows_in.shape
     return pl.pallas_call(
         gram_kernel,
-        out_shape=jax.ShapeDtypeStruct((len(upper_blocks(order)) * B, B), jnp.float32),
+        out_shape=jax.ShapeDtypeStruct((packed_rows(order), B), jnp.float32),
         in_specs=[pl.BlockSpec(memory_space=pltpu.SMEM), WHOLE],
         out_specs=WHOLE,
         scratch_shapes=[
@@ -130,9 +151,14 @@
         for v in range(groups)
     ]
     done = list(rows)
+    pivot = spread(cols[0][0][:1])
     for j in range(NB):
         first, r = divmod(j, SUB)
-        root = lax.rsqrt(spread(cols[j][first][r : r + 1]))
+        root = lax.rsqrt(pivot)
+        if j + 1 < NB:
+            g, q = divmod(j + 1, SUB)
+            ahead = spread(cols[j][g][q : q + 1])
+            pivot = spread(cols[j + 1][g][q : q + 1]) - ahead * ahead * (1.0 / pivot)
         scaled = [None if c is None else c * root for c in cols[j]]
         row = spread(rows[first][r : r + 1]) * root
         done[first] = jnp.where(sub == r, row, done[first])
@@ -172,10 +198,21 @@
 
 def factor(scale, packed_ref, upper_ref, top_ref, low_ref, work):
     order = work.shape[0]
-    for p, (i, j) in enumerate(upper_blocks(order)):
-        work[i * B : (i + 1) * B, j * B : (j + 1) * B] = (
-            packed_ref[p * B : (p + 1) * B, :] * scale
-        )
+    at = 0
+    for i, j in upper_blocks(order):
+        if i != j:
+            work[i * B : (i + 1) * B, j * B : (j + 1) * B] = packed_ref[at : at + B, :] * scale
+            at += B
+    half = B // 2
+    right = lax.broadcasted_iota(jnp.int32, (half, B), 1) >= half
+    for i in range(0, order // B, 2):
+        both = packed_ref[at + B : at + B + half, :] * scale
+        for k, low in ((0, pltpu.roll(both, half, 1)), (1, both)):
+            lo = (i + k) * B
+            span = slice(lo, lo + B)
+            work[lo : lo + half, span] = packed_ref[at + k * half : at + (k + 1) * half, :] * scale
+            work[lo + half : lo + B, span] = jnp.where(right, low, 0.0)
+        at += B + half
     lane = lax.broadcasted_iota(jnp.int32, (B, B), 1)
     sub = lax.broadcasted_iota(jnp.int32, (B, B), 0)
     for s in range(order // B):
@@ -286,7 +323,7 @@
 
 
 def summed(packed):
-    tiles = packed.reshape(lax.axis_size(PLANE), -1, B)
+    tiles = packed.reshape(lax.axis_size(PLANE), -1, SUB // 2, B)
     own = exchanged(tiles, PLANE).sum(axis=0)
     own = everyone(own, "z_low").sum(axis=0)
     own = everyone(own, "z_high").sum(axis=0)

time: 98.1 us -> 96.5 us (0.984)
  blocking collectives: 74.1 us -> 72.7 us
    all_to_all x4, blocking collectives: 74.1 us -> 72.7 us  [exchanged(): return lax.all_to_all(tiles, axis, split_axis=0, concat_axis=0, tiled=True)]
where the time goes in v4:
time: 96.5 us; the launch traced here: 96.2 us
  blocking collectives  72.7 us (75%)
  Pallas kernels  20.2 us (21%)
  local copies, waits for them, and re-layouts  1.7 us (2%)
  between operations  1.32 us (1%)
    all_to_all x4, blocking collectives, exchanged(): return lax.all_to_all(tiles, axis, split_axis=0, concat_axis=0, tiled=True)  72.7 us
    pallas_call x1, Pallas kernels, solved(): pl.pallas_call(functools.partial(solve_kernel, scale), out_shape=[jax.Sha...  16.9 us
    pallas_call x1, Pallas kernels, gram_of(): pl.pallas_call(gram_kernel, out_shape=jax.ShapeDtypeStruct((packed_rows(o...  3.26 us

profile of v4, /device:TPU:1, one launch (start us, length us, event | category | flops | bytes accessed | tf_op | source)
XLA Modules:
  0.0 96.2 jit_solution(9767111725346997209)
XLA Ops:
  1.3 0.1 pad_add_fusion.count_ref.scalars_ref
  1.4 0.0 copy-start
  1.4 1.6 %copy-done = f32[1024,512]{1,0:T(8,128)S(1)} copy-done((f32[1024,512]{1,0:T(8,128)S(1)}, f32[1024,512]{1,0:T(8,128)}, u32[]{:S(2)}) %copy-start) | copy-done | bytes 2097176
  2.9 3.3 %gram.1 = f32[1152,128]{1,0:T(8,128)S(1)} custom-call(s32[2]{0:T(128)S(1)} %pad_add_fusion.count_ref.scalars_ref, f32[1024,512]{1,0:T(8,128)S(1)} %copy-done), custom_call_target="tpu_custom_call" | custom-call | tf_op jit(solution)/shard_map/gram/pallas_call | solution.py:100
  6.2 0.0 copy-start.1
  6.2 21.4 %all_to_all.20 = f32[32,9,4,128]{3,2,1,0:T(4,128)S(1)} all-to-all(f32[32,9,4,128]{3,2,1,0:T(4,128)S(1)} %bitcast.4), channel_id=1, replica_groups=mesh['z_high'=4,'z_low'=4,'core'=2,'y'=4,'x'=4] {'core','y','x'}, dimensions={0} | all-to-all | bytes 1179648 | tf_op jit(solution)/shard_map/all_to_all | solution.py:318
  27.7 0.1 reduce_sum.27
  27.8 8.8 %all_to_all.21 = f32[4,9,4,128]{3,2,1,0:T(4,128)S(1)} all-to-all(f32[4,9,4,128]{3,2,1,0:T(4,128)S(1)} %broadcast_in_dim.9), channel_id=1, replica_groups=mesh['z_high'=4,'z_low'=4,'core'=2,'y'=4,'x'=4] {'z_low'}, dimensions={0} | all-to-all | bytes 147456 | tf_op jit(solution)/shard_map/all_to_all | solution.py:318
  36.7 23.6 %all_to_all.22 = f32[4,9,4,128]{3,2,1,0:T(4,128)S(1)} all-to-all(f32[4,9,4,128]{3,2,1,0:T(4,128)S(1)} %broadcast_in_dim.10), channel_id=1, replica_groups=mesh['z_high'=4,'z_low'=4,'core'=2,'y'=4,'x'=4] {'z_high'}, dimensions={0} | all-to-all | bytes 147456 | tf_op jit(solution)/shard_map/all_to_all | solution.py:318
  60.3 0.1 broadcast_in_dim.11
  60.4 18.8 %all_to_all.23 = f32[32,9,4,128]{3,2,1,0:T(4,128)S(1)} all-to-all(f32[32,9,4,128]{3,2,1,0:T(4,128)S(1)} %broadcast_in_dim.11), channel_id=1, replica_groups=mesh['z_high'=4,'z_low'=4,'core'=2,'y'=4,'x'=4] {'core','y','x'}, dimensions={0} | all-to-all | bytes 1179648 | tf_op jit(solution)/shard_map/all_to_all | solution.py:318
  79.2 0.0 copy-done.1
  79.2 16.9 %solve.1 = (f32[1024,512]{1,0:T(8,128)}, f32[32,512]{1,0:T(8,128)}) custom-call(s32[2]{0:T(128)S(1)} %pad_add_fusion.count_ref.scalars_ref, f32[1152,128]{1,0:T(8,128)S(1)} %bitcast.3, f32[1024,512]{1,0:T(8,128)S(1)} %copy-done.1), custom_call_target="tpu_custom_call" | custom-call | tf_op jit(solution)/shard_map/solve/pallas_call | solution.py:296
  (4 shorter events, 0.1 us)
Async XLA Ops:
  1.4 1.6 %copy-start = (f32[1024,512]{1,0:T(8,128)S(1)}, f32[1024,512]{1,0:T(8,128)}, u32[]{:S(2)}) copy-start(f32[1024,512]{1,0:T(8,128)} %rows_ref.1) | copy-start | bytes 6291460
  6.2 73.0 %copy-start.1 = (f32[1024,512]{1,0:T(8,128)S(1)}, f32[1024,512]{1,0:T(8,128)}, u32[]{:S(2)}) copy-start(f32[1024,512]{1,0:T(8,128)} %rows_ref.1) | copy-start | bytes 6291460

commit v5 on v4

--- a/solution.py
+++ b/solution.py
@@ -50,28 +50,18 @@
     return lax.dot_general(left, right, (dims, ((), ())), preferred_element_type=jnp.float32)
 
 
-def gram_kernel(count_ref, rows, packed_ref, left_sum, right_sum):
-    capacity, order = rows.shape
-    height = capacity // CHUNKS
+def gram_kernel(_, top_ref, low_ref, packed_ref, left_sum, right_sum):
+    order = top_ref.shape[1]
     wide = order // 2
-
-    left_sum[...] = jnp.zeros_like(left_sum)
-    right_sum[...] = jnp.zeros_like(right_sum)
-    row = lax.broadcasted_iota(jnp.int32, (height, order), 0)
-
-    @pl.loop(0, CHUNKS)
-    def _(c):
-        held = rows[pl.ds(pl.multiple_of(c * height, height), height), :]
-        live = jnp.where(row < count_ref[0] - c * height, held, 0.0)
-        top, low = halves(live)
-        top_t, low_t = halves(live.T)
-        for total, side in ((left_sum, slice(0, wide)), (right_sum, slice(wide, order))):
-            tall = total.shape[0]
-            term = narrow_dot(top_t[:tall], top[:, side])
-            term += narrow_dot(low_t[:tall], top[:, side])
-            term += narrow_dot(top_t[:tall], low[:, side])
-            term += narrow_dot(low_t[:tall], low[:, side])
-            total[...] += term
+    top, low = top_ref[...], low_ref[...]
+    top_t, low_t = top.T, low.T
+    for total, side in ((left_sum, slice(0, wide)), (right_sum, slice(wide, order))):
+        tall = total.shape[0]
+        term = narrow_dot(top_t[:tall], top[:, side])
+        term += narrow_dot(low_t[:tall], top[:, side])
+        term += narrow_dot(top_t[:tall], low[:, side])
+        term += narrow_dot(low_t[:tall], low[:, side])
+        total[...] = term
 
     def block(i, j):
         side, inner = divmod(j * B, wide)
@@ -95,12 +85,19 @@
         at += B + half
 
 
-def gram_of(rows_in, count):
-    capacity, order = rows_in.shape
+def live_halves(rows_in, count):
+    row = lax.broadcasted_iota(jnp.int32, rows_in.shape, 0)
+    live = jnp.where(row < count, rows_in, 0.0)
+    rounded = lax.reduce_precision(live, 8, 7)
+    return rounded.astype(jnp.bfloat16), (live - rounded).astype(jnp.bfloat16)
+
+
+def gram_of(index, live_top, live_low):
+    order = live_top.shape[1]
     return pl.pallas_call(
         gram_kernel,
         out_shape=jax.ShapeDtypeStruct((packed_rows(order), B), jnp.float32),
-        in_specs=[pl.BlockSpec(memory_space=pltpu.SMEM), WHOLE],
+        in_specs=[pl.BlockSpec(memory_space=pltpu.SMEM), WHOLE, WHOLE],
         out_specs=WHOLE,
         scratch_shapes=[
             pltpu.VMEM((order // 2, order // 2), jnp.float32),
@@ -108,7 +105,7 @@
         ],
         compiler_params=pltpu.CompilerParams(vmem_limit_bytes=ROOM),
         name="gram",
-    )(count, rows_in)
+    )(index, live_top, live_low)
 
 
 def spread(row):
@@ -257,16 +254,15 @@
 
 
 def solve_kernel(
-    scale, scalars_ref, packed_ref, rows_ref, out_ref, share_ref,
+    scale, index_ref, packed_ref, live_top_ref, live_low_ref, out_ref, share_ref,
     work, upper, top, low, result, sems,
 ):
-    capacity, order = rows_ref.shape
+    capacity, order = live_top_ref.shape
     height = capacity // CHUNKS
     half = order // 2
     factor(scale, packed_ref, upper, top, low, work)
     share = share_ref.shape[0]
-    share_ref[...] = upper[pl.ds(pl.multiple_of(scalars_ref[1] * share, share), share), :]
-    row = lax.broadcasted_iota(jnp.int32, (height, order), 0)
+    share_ref[...] = upper[pl.ds(pl.multiple_of(index_ref[0] * share, share), share), :]
 
     def store(c):
         span = pl.ds(pl.multiple_of(c * height, height), height)
@@ -275,8 +271,7 @@
     @pl.loop(0, CHUNKS)
     def _(c):
         span = pl.ds(pl.multiple_of(c * height, height), height)
-        live = jnp.where(row < scalars_ref[0] - c * height, rows_ref[span, :], 0.0)
-        live_top, live_low = halves(live)
+        live_top, live_low = live_top_ref[span, :], live_low_ref[span, :]
         for k in range(2):
             lo, hi = k * half, (k + 1) * half
             value = narrow_dot(live_top[:, :hi], top[lo:hi, :hi], ((1,), (1,)))
@@ -289,17 +284,17 @@
         store(c).wait()
 
 
-def solved(packed, rows_in, scalars, members, scale):
-    capacity, order = rows_in.shape
+def solved(packed, live_top, live_low, index, members, scale):
+    capacity, order = live_top.shape
     square = pltpu.VMEM((order, order), jnp.float32)
     tall = pltpu.VMEM((capacity, order), jnp.float32)
     return pl.pallas_call(
         functools.partial(solve_kernel, scale),
         out_shape=[
-            jax.ShapeDtypeStruct(rows_in.shape, jnp.float32),
+            jax.ShapeDtypeStruct((capacity, order), jnp.float32),
             jax.ShapeDtypeStruct((order // members, order), jnp.float32),
         ],
-        in_specs=[pl.BlockSpec(memory_space=pltpu.SMEM), WHOLE, WHOLE],
+        in_specs=[pl.BlockSpec(memory_space=pltpu.SMEM), WHOLE, WHOLE, WHOLE],
         out_specs=[FAR, WHOLE],
         scratch_shapes=[
             square,
@@ -311,7 +306,7 @@
         ],
         compiler_params=pltpu.CompilerParams(vmem_limit_bytes=ROOM),
         name="solve",
-    )(scalars, packed, rows_in)
+    )(index, packed, live_top, live_low)
 
 
 def exchanged(tiles, axis):
@@ -334,9 +329,10 @@
     capacity, order = sketch.shape
     members = lax.axis_size(DEV)
     row_total = lax.axis_size(ALL) * HOLD * (capacity // SLOTS)
-    scalars = jnp.stack([row_counts[0], lax.axis_index(DEV)])
-    packed = summed(gram_of(sketch, scalars))
-    return solved(packed, sketch, scalars, members, 1.0 / row_total)
+    index = lax.axis_index(DEV).reshape(1)
+    live_top, live_low = live_halves(sketch, row_counts[0])
+    packed = summed(gram_of(index, live_top, live_low))
+    return solved(packed, live_top, live_low, index, members, 1.0 / row_total)
 
 
 def solution(mesh):

time: 96.5 us -> 94.8 us (0.982)
  Pallas kernels: 20.2 us -> 18.2 us
  other arithmetic: 0.22 us -> 2.1 us
  local copies, waits for them, and re-layouts: 1.7 us -> 0.1 us
    convert_element_type x0 -> x1, other arithmetic: none -> 1.95 us  [live_halves(): return (rounded.astype(jnp.bfloat16), (live - rounded).astype(jnp.bfloat16))]
    unnamed x4 -> x0, local copies, waits for them, and re-layouts: 1.6 us -> none
    pallas_call x1, Pallas kernels: 3.26 us -> 1.86 us  [gram_of(): pl.pallas_call(gram_kernel, out_shape=jax.ShapeDtypeStruct((packed_rows(o...]
where the time goes in v5:
time: 94.8 us; the launch traced here: 94.5 us
  blocking collectives  72.6 us (77%)
  Pallas kernels  18.2 us (19%)
  other arithmetic  2.1 us (2%)
  between operations  1.49 us (2%)
    all_to_all x4, blocking collectives, exchanged(): return lax.all_to_all(tiles, axis, split_axis=0, concat_axis=0, tiled=True)  72.6 us
    pallas_call x1, Pallas kernels, solved(): pl.pallas_call(functools.partial(solve_kernel, scale), out_shape=[jax.Sha...  16.4 us
    convert_element_type x1, other arithmetic, live_halves(): return (rounded.astype(jnp.bfloat16), (live - rounded).astype(jnp.bfloat16))  1.95 us

profile of v5, /device:TPU:1, one launch (start us, length us, event | category | flops | bytes accessed | tf_op | source)
XLA Modules:
  0.0 94.5 jit_solution(2210163106640718126)
XLA Ops:
  1.3 1.9 %fusion = (bf16[1024,512]{1,0:T(8,128)(2,1)S(1)}, bf16[1024,512]{1,0:T(8,128)(2,1)S(1)}) fusion(f32[1024,512]{1,0:T(8,128)} %param.2, pred[1024]{0:T(1024)(128)(4,1)S(1)} %iota_compare_fusion), kind=kLoop, calls=%fused_computation.2 | loop fusion | flops 2621440 | bytes 4195328 | tf_op jit(solution)/shard_map/convert_element_type | solution.py:92
  3.3 1.9 %gram.1 = f32[1152,128]{1,0:T(8,128)S(1)} custom-call(s32[1]{0:T(128)} %bitcast._.index_ref, bf16[1024,512]{1,0:T(8,128)(2,1)S(1)} %get-tuple-element.3.top_ref.live_top_ref, bf16[1024,512]{1,0:T(8,128)(2,1)S(1)} %get-tuple-element.2.low_ref.live_low_ref), custom_call_target="tpu_custom_call" | custom-call | tf_op jit(solution)/shard_map/gram/pallas_call | solution.py:97
  5.1 21.3 %all_to_all.20 = f32[32,9,4,128]{3,2,1,0:T(4,128)S(1)} all-to-all(f32[32,9,4,128]{3,2,1,0:T(4,128)S(1)} %bitcast.6), channel_id=1, replica_groups=mesh['z_high'=4,'z_low'=4,'core'=2,'y'=4,'x'=4] {'core','y','x'}, dimensions={0} | all-to-all | bytes 1179648 | tf_op jit(solution)/shard_map/all_to_all | solution.py:313
  26.4 0.1 reduce_sum.27
  26.5 8.8 %all_to_all.21 = f32[4,9,4,128]{3,2,1,0:T(4,128)S(1)} all-to-all(f32[4,9,4,128]{3,2,1,0:T(4,128)S(1)} %broadcast_in_dim.14), channel_id=1, replica_groups=mesh['z_high'=4,'z_low'=4,'core'=2,'y'=4,'x'=4] {'z_low'}, dimensions={0} | all-to-all | bytes 147456 | tf_op jit(solution)/shard_map/all_to_all | solution.py:313
  35.4 23.6 %all_to_all.22 = f32[4,9,4,128]{3,2,1,0:T(4,128)S(1)} all-to-all(f32[4,9,4,128]{3,2,1,0:T(4,128)S(1)} %broadcast_in_dim.15), channel_id=1, replica_groups=mesh['z_high'=4,'z_low'=4,'core'=2,'y'=4,'x'=4] {'z_high'}, dimensions={0} | all-to-all | bytes 147456 | tf_op jit(solution)/shard_map/all_to_all | solution.py:313
  59.1 0.1 broadcast_in_dim.16
  59.2 18.8 %all_to_all.23 = f32[32,9,4,128]{3,2,1,0:T(4,128)S(1)} all-to-all(f32[32,9,4,128]{3,2,1,0:T(4,128)S(1)} %broadcast_in_dim.16), channel_id=1, replica_groups=mesh['z_high'=4,'z_low'=4,'core'=2,'y'=4,'x'=4] {'core','y','x'}, dimensions={0} | all-to-all | bytes 1179648 | tf_op jit(solution)/shard_map/all_to_all | solution.py:313
  78.0 16.4 %solve.1 = (f32[1024,512]{1,0:T(8,128)}, f32[32,512]{1,0:T(8,128)}) custom-call(s32[1]{0:T(128)} %bitcast._.index_ref, f32[1152,128]{1,0:T(8,128)S(1)} %bitcast.5, bf16[1024,512]{1,0:T(8,128)(2,1)S(1)} %get-tuple-element.3.top_ref.live_top_ref, bf16[1024,512]{1,0:T(8,128)(2,1)S(1)} %get-tuple-element.2.low_ref.live_low_ref), custom_call_target="tpu_custom_call" | custom-call | tf_op jit(solution)/shard_map/solve/pallas_call | solution.py:291
  (5 shorter events, 0.1 us)
